TPU v7x, 256 devices: a whole 4x4x8 slice. The times are simulated.
256 devices in a mesh: cp: 64 (over z_hi, y, x), sp: 4 (over z_lo, core).
Axes of the slice: x: 4, y: 4, z: 8 (z_hi: 4, z_lo: 2; z = z_hi * 2 + z_lo), core: 2. Of those that a mesh axis runs over, the one named last changes fastest.
Arguments:
- queries: bfloat16 [24576, 2048], P(('cp', 'sp')), may hold values from -6 to 6
- key_vectors: bfloat16 [24576, 512], P(('cp', 'sp')), may hold values from -6 to 6
- value_matrix: bfloat16 [24576, 512], P(('cp', 'sp')), may hold values from -6 to 6
- span_order: int32 [64], replicated, may hold values from 0 to 63, each once
Outputs:
- attended: bfloat16 [24576, 2048], P(('cp', 'sp'))
Inputs may be any that keep to these rules, and one draw needn't show every extreme that they name: `span_order`: each value appears exactly once.
All inputs are finite; a program needn't handle non-finite values.
Results may differ from a plain program's by a relative error of at most 0.0055.
Values may be sent and summed in bfloat16 or wider, within the bound.
No kernel may reach another device: no remote copies, remote signals or barrier semaphores. Data moves between devices by JAX's collectives and lax.ppermute only.
A program may use at most 128 MiB of HBM per device.

v0:
```python
import jax
import jax.numpy as jnp
from jax import lax
from jax.sharding import Mesh
from jax.sharding import PartitionSpec as P

HEAD_WIDTH = 128
SP = ("sp_0", "sp_1")
CP_SP = ("cp", "sp_0", "sp_1")


masked_score = -1e30


def sent_together(arrays, axis, dim, along):
    both = jnp.concatenate(arrays, axis=along)
    out, at, done = (lax.all_gather(both, axis, axis=dim, tiled=True), 0, [])
    for a in arrays:
        done.append(lax.slice_in_dim(out, at, at + a.shape[along], axis=along))
        at += a.shape[along]
    return tuple(done)


def in_blocks(x, dim, devices):
    lengths = x.shape
    blocks = x.reshape(*lengths[:dim], devices, lengths[dim] // devices, *lengths[dim + 1 :])
    return jnp.moveaxis(blocks, dim, 0)


def laid_out(blocks, dim):
    blocks = jnp.moveaxis(blocks, 0, dim)
    lengths = blocks.shape
    return blocks.reshape(*lengths[:dim], lengths[dim] * lengths[dim + 1], *lengths[dim + 2 :])


def moved_by_axis(blocks, axes, order):
    inside = blocks.shape[1:]
    out = blocks.reshape(*(lax.axis_size(a) for a in axes), *inside)
    for k in order:
        out = lax.all_to_all(out, axes[k], k, k, tiled=True)
    return out.reshape(-1, *inside)


def core_and_chips(x, groups, order, split_dim, concat_dim):
    devices = lax.axis_size(groups[0]) * lax.axis_size(groups[1])
    blocks = in_blocks(x, split_dim, devices)
    return laid_out(moved_by_axis(blocks, groups, order), concat_dim)


def span_position(row_ids, span_order, pair_count, span_rows):
    slot_ids = row_ids // span_rows
    pair_ids = slot_ids // 2
    picked = jnp.sum(
        jnp.where(
            pair_ids[:, None] == jnp.arange(pair_count, dtype=jnp.int32)[None, :],
            span_order[None, :],
            0,
        ),
        axis=1,
    )
    span_ids = jnp.where(slot_ids % 2 == 1, 2 * pair_count - 1 - picked, picked)
    return span_ids * span_rows + row_ids % span_rows


def absorb_block(state_in, query_blk, query_pos, key_blk, value_blk, key_pos):
    run_max, run_sum, accumulated = state_in
    scores = jnp.einsum(
        "qhd,kd->hqk", query_blk, key_blk, preferred_element_type=jnp.float32
    ) * query_blk.shape[2] ** (-0.5)
    allowed = key_pos[None, None, :] <= query_pos[None, :, None]
    new_peak = jnp.maximum(run_max, jnp.max(jnp.where(allowed, scores, masked_score), axis=2))
    weights = jnp.where(allowed, jnp.exp(scores - new_peak[:, :, None]), 0.0)
    factor = jnp.exp(run_max - new_peak)
    run_sum = run_sum * factor + jnp.sum(weights, axis=2)
    accumulated = accumulated * factor[:, :, None] + jnp.einsum(
        "hqk,kd->hqd", weights.astype(jnp.bfloat16), value_blk, preferred_element_type=jnp.float32
    )
    return (new_peak, run_sum, accumulated)


def pick_block(key_count, unit_rows):
    block_row_list = unit_rows
    while block_row_list * 2 <= 1024 and key_count % (block_row_list * 2) == 0:
        block_row_list = block_row_list * 2
    return block_row_list


def guarded(state_in, query_blk, query_pos, key_blk, value_blk, key_pos, lowest):

    def compute(states):
        return absorb_block(states, query_blk, query_pos, key_blk, value_blk, key_pos)

    def unchanged(states):
        return states

    return lax.cond(lowest <= jnp.max(query_pos), compute, unchanged, state_in)


def sweep(carries, query_list, key_rows, value_rows, position_of, block_row_list):
    key_count = key_rows.shape[0]

    def advance(states, offset):
        key_blk = lax.dynamic_slice_in_dim(key_rows, offset, block_row_list, 0)
        value_blk = lax.dynamic_slice_in_dim(value_rows, offset, block_row_list, 0)
        key_pos = position_of(offset + jnp.arange(block_row_list, dtype=jnp.int32))
        lowest = jnp.min(key_pos)
        updated = []
        for state_in, entry in zip(states, query_list):
            updated.append(
                guarded(state_in, entry[0], entry[1], key_blk, value_blk, key_pos, lowest)
            )
        return (tuple(updated), None)

    offsets = jnp.arange(key_count // block_row_list, dtype=jnp.int32) * block_row_list
    return lax.scan(advance, carries, offsets)[0]


def per_device(queries, key_vectors, value_matrix, span_order):
    tok_rows = queries.shape[0]
    cp_count = lax.axis_size("cp")
    sp_count = lax.axis_size(SP)
    local_query = lax.all_to_all(queries, SP, split_axis=1, concat_axis=0, tiled=True)
    group_rows = local_query.shape[0]
    span_rows = group_rows // 2
    head_count = local_query.shape[1] // HEAD_WIDTH
    query_heads = local_query.reshape(group_rows, head_count, HEAD_WIDTH)
    group_id = lax.axis_index("cp")
    query_ids = group_id * group_rows + jnp.arange(group_rows, dtype=jnp.int32)
    query_pos = span_position(query_ids, span_order, cp_count, span_rows)
    query_list = [
        (query_heads[:span_rows], query_pos[:span_rows]),
        (query_heads[span_rows:], query_pos[span_rows:]),
    ]
    initial = tuple(
        (
            (
                jnp.full((head_count, entry[1].shape[0]), masked_score, jnp.float32),
                jnp.zeros((head_count, entry[1].shape[0]), jnp.float32),
                jnp.zeros((head_count, entry[1].shape[0], HEAD_WIDTH), jnp.float32),
            )
            for entry in query_list
        )
    )
    whole_key, whole_value = sent_together((key_vectors, value_matrix), "cp", 0, 1)
    head_key, head_value = (
        lax.all_to_all(whole_key, SP, split_axis=1, concat_axis=0, tiled=True),
        lax.all_to_all(whole_value, SP, split_axis=1, concat_axis=0, tiled=True),
    )
    total_rows = head_key.shape[0]
    span_count = total_rows // span_rows
    slot_ids = jnp.arange(span_count, dtype=jnp.int32)
    pair_pick = jnp.sum(
        jnp.where(
            (slot_ids // 2)[:, None] == jnp.arange(cp_count, dtype=jnp.int32)[None, :],
            span_order[None, :],
            0,
        ),
        axis=1,
    )
    span_of_slot = jnp.where(slot_ids % 2 == 1, 2 * cp_count - 1 - pair_pick, pair_pick)
    slot_of_span = jnp.sum(
        jnp.where(span_of_slot[None, :] == slot_ids[:, None], slot_ids[None, :], 0), axis=1
    )

    def position_layout(rows):
        stored = jnp.transpose(rows.reshape(sp_count, cp_count, tok_rows, HEAD_WIDTH), (1, 0, 2, 3))
        spans = stored.reshape(span_count, span_rows, HEAD_WIDTH)
        return jnp.take(spans, slot_of_span, axis=0).reshape(total_rows, HEAD_WIDTH)

    ordered_key = position_layout(head_key)
    ordered_value = position_layout(head_value)

    def plain_position(row_ids):
        return row_ids

    carries = sweep(
        initial,
        query_list,
        ordered_key,
        ordered_value,
        plain_position,
        pick_block(total_rows, span_rows),
    )
    pieces = [entry[2] / entry[1][:, :, None] for entry in carries]
    joined = jnp.concatenate(pieces, axis=1)
    mixed_rows = (
        jnp.transpose(joined, (1, 0, 2))
        .reshape(group_rows, head_count * HEAD_WIDTH)
        .astype(jnp.bfloat16)
    )
    return core_and_chips(mixed_rows, ("sp_0", "sp_1"), (1, 0), 0, 1)


def solution(mesh):
    finer = Mesh(mesh.devices.reshape(mesh.shape["cp"], 2, 2), ("cp", "sp_0", "sp_1"))
    in_specs = (P(CP_SP, None), P(CP_SP, None), P(CP_SP, None), P())
    out_specs = P(CP_SP, None)
    return jax.shard_map(
        per_device, mesh=finer, in_specs=in_specs, out_specs=out_specs, check_vma=False
    )
```

profile of v0, /device:TPU:1, one launch (start us, length us, event | category | flops | bytes accessed | tf_op | source)
XLA Modules:
  0.0 708.4 jit_solution(12042619785912234587)
XLA Ops:
  6.5 1.6 pad_maximum_fusion
  8.2 1.8 copy.82
  10.0 6.6 all-to-all-start.2
  16.6 125.1 %all-gather.2.cloned.1.call-done = bf16[6144,1024]{1,0:T(8,128)(2,1)} async-done(((bf16[96,1024]{1,0:T(8,128)(2,1)}), bf16[6144,1024]{1,0:T(8,128)(2,1)}) %all-gather.2.cloned.1.call-update) | async-done | bytes 12582928 | tf_op jit(solution)/shard_map/all_gather | solution.py:17
  141.7 10.2 %fusion.38 = (bf16[6144,512]{1,0:T(8,128)(2,1)}, bf16[6144,512]{1,0:T(8,128)(2,1)}) fusion(bf16[6144,1024]{1,0:T(8,128)(2,1)} %all-gather.2.cloned.1.call-done), kind=kLoop, calls=%fused_computation.90 | loop fusion | bytes 25165824 | tf_op jit(solution)/shard_map/slice | solution.py:19
  151.9 8.7 %copy.77 = bf16[6144,512]{0,1:T(8,128)(2,1)} copy(bf16[6144,512]{1,0:T(8,128)(2,1)} %get-tuple-element.375) | data formatting | bytes 12582912
  160.6 17.6 %all-to-all-start = ((bf16[6144,4,128]{0,2,1:T(8,128)(2,1)}), bf16[6144,4,128]{0,2,1:T(8,128)(2,1)}, u32[]{:S(2)}, u32[]{:S(2)}) async-start(bf16[6144,4,128]{0,2,1:T(8,128)(2,1)} %bitcast.76), calls=%async_computation | async-start | bytes 12582912 | tf_op jit(solution)/shard_map/all_to_all | solution.py:146
  178.3 8.7 %copy.78 = bf16[6144,512]{0,1:T(8,128)(2,1)} copy(bf16[6144,512]{1,0:T(8,128)(2,1)} %get-tuple-element.374) | data formatting | bytes 12582912
  187.0 62.3 %all-to-all-done = bf16[6144,4,128]{0,2,1:T(8,128)(2,1)} async-done(((bf16[6144,4,128]{0,2,1:T(8,128)(2,1)}), bf16[6144,4,128]{0,2,1:T(8,128)(2,1)}, u32[]{:S(2)}, u32[]{:S(2)}) %all-to-all-start) | async-done | bytes 6291488 | tf_op jit(solution)/shard_map/all_to_all | solution.py:146
  249.3 6.6 all-to-all-start.1
  257.2 8.7 %copy.65 = bf16[4,6144,128]{2,1,0:T(8,128)(2,1)} copy(bf16[4,6144,128]{1,2,0:T(8,128)(2,1)} %bitcast.8) | data formatting | bytes 12582912 | tf_op jit(solution)/shard_map/all_to_all | solution.py:146
  265.9 7.4 %copy.66 = bf16[64,4,96,128]{3,2,1,0:T(8,128)(2,1)} copy(bf16[64,4,96,128]{3,2,0,1:T(8,128)(2,1)} %bitcast.79) | data formatting | bytes 12582912 | tf_op jit(solution)/shard_map/transpose | solution.py:166
  273.2 52.4 %all-to-all-done.1 = bf16[6144,4,128]{0,2,1:T(8,128)(2,1)} async-done(((bf16[6144,4,128]{0,2,1:T(8,128)(2,1)}), bf16[6144,4,128]{0,2,1:T(8,128)(2,1)}, u32[]{:S(2)}, u32[]{:S(2)}) %all-to-all-start.1) | async-done | bytes 6291488 | tf_op jit(solution)/shard_map/all_to_all | solution.py:147
  325.6 8.7 %copy.68 = bf16[4,6144,128]{2,1,0:T(8,128)(2,1)} copy(bf16[4,6144,128]{1,2,0:T(8,128)(2,1)} %bitcast.14) | data formatting | bytes 12582912 | tf_op jit(solution)/shard_map/all_to_all | solution.py:147
  334.3 7.4 %copy.69 = bf16[64,4,96,128]{3,2,1,0:T(8,128)(2,1)} copy(bf16[64,4,96,128]{3,2,0,1:T(8,128)(2,1)} %bitcast.80) | data formatting | bytes 12582912 | tf_op jit(solution)/shard_map/transpose | solution.py:166
  341.7 6.8 gather_fusion
  348.5 6.7 gather_fusion.1
  355.2 10.4 %broadcast_select_fusion = (bf16[128,192,128]{2,1,0:T(8,128)(2,1)}, bf16[128,192,128]{2,1,0:T(8,128)(2,1)}) fusion(bf16[128,192,128]{2,1,0:T(8,128)(2,1)} %gather_fusion.1, pred[128]{0:T(512)(128)(4,1)S(1)} %compare_and_fusion, bf16[128,192,128]{2,1,0:T(8,128)(2,1)} %gather_fusion), kind=kLoop, calls=%fused_computation.44 | loop fusion | flops 6291456 | bytes 25165952 | tf_op jit(solution)/shard_map/jit(_take)/select_n | solution.py:168
  365.7 320.8 %while.21 = (s32[]{:T(128)}, f32[4,192]{1,0:T(4,128)S(1)}, f32[4,192]{1,0:T(4,128)S(1)}, f32[4,192,128]{2,1,0:T(8,128)S(1)}, f32[4,192]{1,0:T(4,128)S(1)}, /*ind...) while((s32[]{:T(128)}, f32[4,192]{1,0:T(4,128)S(1)}, ...), condition=%wide.region_15.17_spmd, body=%wide.region_5.16_spmd.sunk | while | flops 617648640 | bytes 18983924 | solution.py:115
  369.4 1.3 iota_add_fusion.3
  371.9 2.6 conditional.5
  375.6 2.6 conditional.4
  382.0 1.3 iota_add_fusion.3
  384.4 2.6 conditional.5
  388.2 2.6 conditional.4
  397.0 2.6 conditional.5
  400.8 2.6 conditional.4
  409.6 2.6 conditional.5
  413.3 2.6 conditional.4
  422.1 2.6 conditional.5
  429.6 1.3 iota_add_fusion.3
  432.0 2.6 conditional.5
  442.0 2.6 conditional.5
  451.9 2.6 conditional.5
  461.9 2.6 conditional.5
  471.8 2.6 conditional.5
  479.3 1.3 iota_add_fusion.3
  481.8 2.6 conditional.5
  489.2 1.3 iota_add_fusion.3
  491.7 2.6 conditional.5
  501.7 2.6 conditional.5
  511.6 2.6 conditional.5
  521.6 2.6 conditional.5
  531.5 2.6 conditional.5
  539.0 1.3 iota_add_fusion.3
  541.4 2.6 conditional.5
  548.9 1.3 iota_add_fusion.3
  551.4 2.6 conditional.5
  561.3 2.6 conditional.5
  571.3 2.6 conditional.5
  581.2 2.6 conditional.5
  591.2 2.6 conditional.5
  598.6 1.3 iota_add_fusion.3
  601.1 2.6 conditional.5
  608.6 1.3 iota_add_fusion.3
  611.1 2.6 conditional.5
  621.0 2.6 conditional.5
  631.0 2.6 conditional.5
  640.9 2.6 conditional.5
  650.8 2.6 conditional.5
  658.3 1.3 iota_add_fusion.3
  660.8 2.6 conditional.5
  687.4 4.7 all_to_all.58
  692.1 8.7 %all_to_all.59 = bf16[2,2,96,512]{3,2,1,0:T(8,128)(2,1)S(1)} all-to-all(bf16[2,2,96,512]{3,2,1,0:T(8,128)(2,1)S(1)} %copy.75), channel_id=1, replica_groups=mesh['cp'=64,'sp_0'=2,'sp_1'=2] {'sp_0'}, dimensions={0} | all-to-all | bytes 786432 | tf_op jit(solution)/shard_map/all_to_all | solution.py:40
  (383 shorter events, 172.7 us)
Async XLA Ops:
  6.5 135.2 %all-gather.2.cloned.1.call-start = ((), (), s32[]{:S(2)}) async-start(), calls=%async_computation.5 | async-start | bytes 12779520 | tf_op jit(solution)/shard_map/all_gather | solution.py:17
  10.0 150.6 %all-to-all-start.2 = ((bf16[96,4,512]{2,0,1:T(8,128)(2,1)}), bf16[96,4,512]{2,0,1:T(8,128)(2,1)S(1)}, u32[]{:S(2)}, u32[]{:S(2)}) async-start(bf16[96,4,512]{2,0,1:T(8,128)(2,1)} %bitcast.72), calls=%async_computation.2 | async-start | bytes 786432 | tf_op jit(solution)/shard_map/all_to_all | solution.py:122
  160.6 88.6 %all-to-all-start = ((bf16[6144,4,128]{0,2,1:T(8,128)(2,1)}), bf16[6144,4,128]{0,2,1:T(8,128)(2,1)}, u32[]{:S(2)}, u32[]{:S(2)}) async-start(bf16[6144,4,128]{0,2,1:T(8,128)(2,1)} %bitcast.76), calls=%async_computation | async-start | bytes 12582912 | tf_op jit(solution)/shard_map/all_to_all | solution.py:146
  249.3 6.7 copy-start
  249.3 76.4 %all-to-all-start.1 = ((bf16[6144,4,128]{0,2,1:T(8,128)(2,1)}), bf16[6144,4,128]{0,2,1:T(8,128)(2,1)}, u32[]{:S(2)}, u32[]{:S(2)}) async-start(bf16[6144,4,128]{0,2,1:T(8,128)(2,1)} %bitcast.75), calls=%async_computation.1 | async-start | bytes 12582912 | tf_op jit(solution)/shard_map/all_to_all | solution.py:147
Sparse Core Ops, SparseCore 0:
  10.5 131.1 all-gather.1
where the time goes:
time: 713 us; the launch traced here: 708 us
  waiting for transfers between devices  240 us (34%)
  loops' own time  139 us (19%)
  local copies, waits for them, and re-layouts  133 us (19%)
  other arithmetic  85.1 us (12%)
  matrix products  54.4 us (8%)
  starting transfers between devices  30.9 us (4%)
  between operations  13.6 us (2%)
  blocking collectives  13.4 us (2%)
    another operation x1, loops' own time, sweep(): return lax.scan(advance, carries, offsets)[0]  137 us
    all_gather x1, waiting for transfers between devices, sent_together(): out, at, done = (lax.all_gather(both, axis, axis=dim, tiled=True), 0, [])  125 us
    all_to_all x1, waiting for transfers between devices, per_device(): lax.all_to_all(whole_key, SP, split_axis=1, concat_axis=0, tiled=True)  62.3 us
    all_to_all x1, waiting for transfers between devices, per_device(): lax.all_to_all(whole_value, SP, split_axis=1, concat_axis=0, tiled=True)  52.4 us
    add x32, other arithmetic, advance(): key_pos = position_of(offset + jnp.arange(block_row_list, dtype=jnp.int32))  40.7 us
    dynamic_slice x32, local copies, waits for them, and re-layouts, advance(): value_blk = lax.dynamic_slice_in_dim(value_rows, offset, block_row_list, 0)  36.4 us
    dot_general x33, matrix products, absorb_block(): jnp.einsum('hqk,kd->hqd', weights.astype(jnp.bfloat16), value_blk, prefer...  31.9 us
    reduce_sum x33, other arithmetic, absorb_block(): run_sum = run_sum * factor + jnp.sum(weights, axis=2)  25.3 us
  transfers between devices with their start and end apart: 4, of which 3 were waited for; matrix products, arithmetic and copies ran while one was open for 7% of the time, Pallas kernels for 0%

commit v1 on v0

v1 whole, which is shorter than its diff:
```python
import jax
import jax.numpy as jnp
from jax import lax
from jax.experimental import pallas as pl
from jax.experimental.pallas import tpu as pltpu
from jax.sharding import Mesh
from jax.sharding import PartitionSpec as P

D = 128
HEADS = 4
AXES = ("zh", "y", "x", "zl", "c")
LOG2E = 1.4426950408889634
LOW = -1e30
NB = 5
CHUNKS = 2
ROWS_O = 136
VMEM = pl.BlockSpec(memory_space=pltpu.VMEM)
SMEM = pl.BlockSpec(memory_space=pltpu.SMEM)


def params():
    return pltpu.CompilerParams(vmem_limit_bytes=48 * 1024 * 1024)


def prep_kernel(q_ref, out_ref):
    for h in range(4):
        cols = [q_ref[:, pl.ds((h * HEADS + j) * D, D)] for j in range(HEADS)]
        stacked = jnp.concatenate(cols, axis=0).astype(jnp.float32)
        out_ref[h] = jnp.transpose(stacked).astype(jnp.bfloat16)


def prep(queries):
    tok = queries.shape[0]
    return pl.pallas_call(
        prep_kernel,
        out_shape=jax.ShapeDtypeStruct((4, D, HEADS * tok), jnp.bfloat16),
        in_specs=[VMEM],
        out_specs=VMEM,
        compiler_params=params(),
        name="prep_q",
    )(queries)


def make_attend(first, last, piece_rows, span_rows, n_pieces, units):
    width = units[0]
    tiles = 2 * width // 256

    def kernel(*refs):
        tab, spans, nfull, nall, qspan, koff, tok, qa, qb, kv = refs[:10]
        rest = refs[10:]
        if not first:
            acc_in, m_in, l_in = rest[:3]
            rest = rest[3:]
        if last:
            own_ref, other_ref, acc, m, l = rest
        else:
            acc, m, l = rest

        def q_tile(j, t):
            lo = t * 256
            if lo + 256 <= width:
                return qa[j, :, lo : lo + 256]
            if lo >= width:
                return qb[j, :, lo - width : lo - width + 256]
            return jnp.concatenate([qa[j, :, lo:], qb[j, :, : 256 - (width - lo)]], axis=1)

        def block(j, base, masked):
            rows = [pl.ds(pl.multiple_of(tab[base + i] * piece_rows, 16), piece_rows) for i in range(NB)]
            keys = jnp.concatenate([kv[r, 0:D] for r in rows], axis=0)
            vals = jnp.concatenate([kv[r, D : 2 * D] for r in rows], axis=0)
            if masked:
                within = lax.broadcasted_iota(jnp.int32, (piece_rows, 256), 0) + koff[0]
                kpos = jnp.concatenate([within + spans[base + i] * span_rows for i in range(NB)], axis=0)
            for t in range(tiles):
                cs = pl.ds(t * 256, 256)
                s = jnp.dot(keys, q_tile(j, t), preferred_element_type=jnp.float32) * (LOG2E * D**-0.5)
                if masked:
                    ok = kpos <= tok[:, cs] + qspan[j] * span_rows
                    s = jnp.where(ok, s, LOW)
                m_old = m[j, :, cs]
                m_new = jnp.maximum(m_old, jnp.max(s, axis=0, keepdims=True))
                alpha = jnp.exp2(m_old - m_new)
                p = jnp.exp2(s - m_new)
                if masked:
                    p = jnp.where(ok, p, 0.0)
                l[j, :, cs] = l[j, :, cs] * alpha + jnp.sum(p, axis=0, keepdims=True)
                m[j, :, cs] = m_new
                pv = lax.dot_general(
                    vals, p.astype(jnp.bfloat16), (((0,), (0,)), ((), ())), preferred_element_type=jnp.float32
                )
                acc[j, :, cs] = acc[j, :, cs] * alpha + pv

        def one_span(j, carry):
            if first:
                acc[j] = jnp.zeros(acc.shape[1:], jnp.float32)
                m[j] = jnp.full(m.shape[1:], LOW, jnp.float32)
                l[j] = jnp.zeros(l.shape[1:], jnp.float32)
            else:
                acc[j] = acc_in[j]
                m[j] = m_in[j]
                l[j] = l_in[j]
            full = nfull[j] // NB

            def step(b, c):
                block(j, b * NB, False)
                return c

            lax.fori_loop(0, full, step, 0)

            @pl.when(nall[j] > full * NB)
            def _():
                block(j, full * NB, True)

            if last:
                total = l[j]
                seen = total > 0.0
                safe = jnp.where(seen, total, 1.0)
                lse = jnp.where(seen, m[j] + jnp.log2(safe), LOW)
                inv = 1.0 / safe
                hi = lse.astype(jnp.bfloat16)
                r1 = lse - hi.astype(jnp.float32)
                mid = r1.astype(jnp.bfloat16)
                low = (r1 - mid.astype(jnp.float32)).astype(jnp.bfloat16)
                stat = jnp.concatenate(
                    [hi.astype(jnp.float32), mid.astype(jnp.float32), low.astype(jnp.float32), jnp.zeros((5, 2 * width), jnp.float32)], axis=0
                ).astype(jnp.bfloat16)
                for ref, lo in ((own_ref, 0), (other_ref, width)):
                    cs = pl.ds(lo, width)
                    ref[j, 0:D] = (acc[j, :, cs] * inv[:, lo : lo + width]).astype(jnp.bfloat16)
                    ref[j, D:ROWS_O] = stat[:, lo : lo + width]
            return carry

        lax.fori_loop(0, qa.shape[0], one_span, 0)

    return kernel


def attend(tables, qa, qb, kv, state, last, piece_rows, span_rows):
    first = state is None
    n_q, _, width = qa.shape
    state_shapes = [
        ((n_q, D, 2 * width), jnp.float32),
        ((n_q, 1, 2 * width), jnp.float32),
        ((n_q, 1, 2 * width), jnp.float32),
    ]
    if last:
        out_shape = [jax.ShapeDtypeStruct((n_q, ROWS_O, width), jnp.bfloat16)] * 2
        scratch = [pltpu.VMEM(s, d) for s, d in state_shapes]
    else:
        out_shape = [jax.ShapeDtypeStruct(s, d) for s, d in state_shapes]
        scratch = []
    args = list(tables) + [qa, qb, kv] + ([] if first else list(state))
    flops = 2 * 2 * n_q * 2 * width * D * kv.shape[0] // 2
    return pl.pallas_call(
        make_attend(first, last, piece_rows, span_rows, kv.shape[0] // piece_rows, (width,)),
        out_shape=out_shape,
        in_specs=[SMEM] * 6 + [VMEM] * (len(args) - 6),
        out_specs=[VMEM] * len(out_shape),
        scratch_shapes=scratch,
        compiler_params=params(),
        cost_estimate=pl.CostEstimate(flops=flops * 2, bytes_accessed=kv.size * 2, transcendentals=0),
        name="attend_last" if last else "attend_more",
    )(*args)


def weights_of(a, b):
    def lse(ref):
        return ref[D : D + 1].astype(jnp.float32) + ref[D + 1 : D + 2].astype(jnp.float32) + ref[D + 2 : D + 3].astype(jnp.float32)

    la, lb = lse(a), lse(b)
    top = jnp.maximum(la, lb)
    ea, eb = jnp.exp2(la - top), jnp.exp2(lb - top)
    total = ea + eb
    return ea / total, eb / total, top + jnp.log2(total)


def combine_kernel(a_ref, b_ref, keep_ref, send_ref):
    half = keep_ref.shape[0]
    for j in range(a_ref.shape[0]):
        wa, wb, lse = weights_of(a_ref[j], b_ref[j])
        mixed = a_ref[j, 0:D].astype(jnp.float32) * wa + b_ref[j, 0:D].astype(jnp.float32) * wb
        hi = lse.astype(jnp.bfloat16).astype(jnp.float32)
        mid = (lse - hi).astype(jnp.bfloat16).astype(jnp.float32)
        low = lse - hi - mid
        stat = jnp.concatenate([hi, mid, low, jnp.zeros((5, lse.shape[1]), jnp.float32)], axis=0)
        ref = keep_ref if j < half else send_ref
        ref[j % half, 0:D] = mixed.astype(jnp.bfloat16)
        ref[j % half, D:ROWS_O] = stat.astype(jnp.bfloat16)


def combine(a, b):
    n = a.shape[0] // 2
    shape = jax.ShapeDtypeStruct((n,) + a.shape[1:], jnp.bfloat16)
    return pl.pallas_call(
        combine_kernel,
        out_shape=[shape, shape],
        in_specs=[VMEM] * 2,
        out_specs=[VMEM] * 2,
        compiler_params=params(),
        name="combine_cores",
    )(a, b)


def finish_kernel(a_ref, b_ref, out_ref):
    tok = out_ref.shape[1]
    for j in range(a_ref.shape[0]):
        wa, wb, _ = weights_of(a_ref[j], b_ref[j])
        mixed = a_ref[j, 0:D].astype(jnp.float32) * wa + b_ref[j, 0:D].astype(jnp.float32) * wb
        rows = jnp.transpose(mixed).astype(jnp.bfloat16)
        for h in range(HEADS):
            out_ref[j, :, pl.ds(h * D, D)] = rows[h * tok : (h + 1) * tok]


def finish(a, b):
    tok = a.shape[2] // HEADS
    return pl.pallas_call(
        finish_kernel,
        out_shape=jax.ShapeDtypeStruct((a.shape[0], tok, HEADS * D), jnp.bfloat16),
        in_specs=[VMEM] * 2,
        out_specs=VMEM,
        compiler_params=params(),
        name="combine_chips",
    )(a, b)


def swap(x, axis):
    return lax.ppermute(x, axis, [(0, 1), (1, 0)])


def exchange(x, axes):
    return lax.all_to_all(x, axes, split_axis=0, concat_axis=0, tiled=True)


def per_device(queries, key_vectors, value_matrix, span_order):
    tok = queries.shape[0]
    pairs = span_order.shape[0]
    span_rows = 2 * tok
    piece = tok // 2
    yx = lax.axis_size("y") * lax.axis_size("x")
    zl, c = lax.axis_index("zl"), lax.axis_index("c")
    mine = lax.axis_index("y") * lax.axis_size("x") + lax.axis_index("x")

    kv = jnp.stack([key_vectors.reshape(tok, 4, D), value_matrix.reshape(tok, 4, D)], axis=2).reshape(2, piece, 4, 2 * D)
    kv = jnp.transpose(kv, (2, 0, 1, 3)).reshape(8, piece, 2 * D)
    column = exchange(kv, ("zh", "zl"))

    q_t = exchange(prep(queries), "zh")
    q_near = jnp.concatenate([q_t, swap(q_t, "zl")], axis=0)
    q_far = swap(q_near, "c")

    per = 8 // CHUNKS
    order = span_order.astype(jnp.int32).reshape(4, yx)
    piece_span = jnp.stack([order, 2 * pairs - 1 - order], axis=1).reshape(CHUNKS, per, yx)
    piece_span = jnp.transpose(piece_span, (0, 2, 1)).reshape(CHUNKS, per * yx)
    count = per * yx
    ids = jnp.arange(count, dtype=jnp.int32)
    rank = jnp.sum((piece_span[:, None, :] < piece_span[:, :, None]).astype(jnp.int32), axis=2)
    hit = rank[:, None, :] == ids[None, :, None]
    tab = jnp.sum(jnp.where(hit, ids[None, None, :], 0), axis=2)
    spans = jnp.sum(jnp.where(hit, piece_span[:, None, :], 0), axis=2)
    tab = jnp.pad(tab, ((0, 0), (0, NB)))
    spans = jnp.pad(spans, ((0, 0), (0, NB)), constant_values=1 << 16)
    here = jnp.sum(jnp.where(jnp.arange(yx, dtype=jnp.int32)[None, :] == mine, order, 0), axis=1)
    early, late = here, 2 * pairs - 1 - here
    q_span = jnp.concatenate([jnp.where(zl == 0, early, late), jnp.where(zl == 0, late, early)])
    nfull = jnp.sum((piece_span[:, None, :] < q_span[None, :, None]).astype(jnp.int32), axis=2)
    nall = jnp.sum((piece_span[:, None, :] <= q_span[None, :, None]).astype(jnp.int32), axis=2)
    koff = (c * tok + zl * piece).astype(jnp.int32).reshape(1)
    cols = jnp.arange(2 * HEADS * tok, dtype=jnp.int32)
    side = jnp.where(cols < HEADS * tok, c, 1 - c)
    token = (cols % tok + side * tok).astype(jnp.int32)[None, :]

    state = None
    for k in range(CHUNKS):
        rows = column[k * per : (k + 1) * per].reshape(1, per * piece, 2 * D)
        gathered = exchange(jnp.broadcast_to(rows, (yx, per * piece, 2 * D)), ("y", "x"))
        gathered = gathered.reshape(yx * per * piece, 2 * D)
        tables = (tab[k], spans[k], nfull[k], nall[k], q_span, koff)
        state = attend(tables + (token,), q_near, q_far, gathered, state, k == CHUNKS - 1, piece, span_rows)
    own, other = state
    keep, send = combine(own, swap(other, "c"))
    done = finish(keep, swap(send, "zl"))
    back = exchange(done, "zh")
    return jnp.transpose(back, (1, 0, 2)).reshape(tok, 4 * HEADS * D)


def solution(mesh):
    finer = Mesh(mesh.devices.reshape(4, 4, 4, 2, 2), AXES)
    spec = P(AXES, None)
    return jax.shard_map(
        per_device, mesh=finer, in_specs=(spec, spec, spec, P()), out_specs=spec, check_vma=False
    )
```

time: 713 us -> 220 us (0.31)
  waiting for transfers between devices: 240 us -> 42.2 us
  loops' own time: 139 us -> 0 us
  local copies, waits for them, and re-layouts: 133 us -> 8.37 us
  Pallas kernels: 0 us -> 115 us
  other arithmetic: 85.1 us -> 1.18 us
  matrix products: 54.4 us -> 0 us
  between operations: 13.6 us -> 0.16 us
    another operation x65 -> x0, loops' own time: 139 us -> none  [the longest x1 137 us: sweep(): return lax.scan(advance, carries, offsets)[0]]
    all_gather x1 -> x0, waiting for transfers between devices: 125 us -> none  [sent_together(): out, at, done = (lax.all_gather(both, axis, axis=dim, tiled=True), 0, [])]
    pallas_call x0 -> x5, Pallas kernels: none -> 115 us  [the longest x2 113 us: attend(): pl.pallas_call(make_attend(first, last, piece_rows, span_rows, kv.shape[0...]
    all_to_all x3 -> x4, waiting for transfers between devices: 115 us -> 24 us  [exchange(): return lax.all_to_all(x, axes, split_axis=0, concat_axis=0, tiled=True)]
    dynamic_slice x64 -> x0, local copies, waits for them, and re-layouts: 56 us -> none  [the longest x32 36.4 us: advance(): value_blk = lax.dynamic_slice_in_dim(value_rows, offset, block_row_list, 0)]
    dot_general x66 -> x0, matrix products: 54.4 us -> none  [the longest x33 31.9 us: absorb_block(): jnp.einsum('hqk,kd->hqd', weights.astype(jnp.bfloat16), value_blk, prefer...]
    add x66 -> x1, other arithmetic: 41.2 us -> 0.02 us  [per_device(): token = (cols % tok + side * tok).astype(jnp.int32)[None, :]]
    reduce_sum x36 -> x4, other arithmetic: 25.6 us -> 0.65 us  [the longest x1 0.21 us: per_device(): jnp.sum((piece_span[:, None, :] <= q_span[None, :, None]).astype(jnp.int3...]
  transfers between devices with their start and end apart: 4 -> 8, of which waited for: 3 -> 6; matrix products, arithmetic and copies ran while one was open for 7% -> 2% of each run, Pallas kernels for 0% -> 26%
where the time goes in v1:
time: 220 us; the launch traced here: 217 us
  Pallas kernels  115 us (52%)
  waiting for transfers between devices  42.2 us (19%)
  starting transfers between devices  34.3 us (16%)
  blocking collectives  16.5 us (8%)
  local copies, waits for them, and re-layouts  8.37 us (4%)
    pallas_call x2, Pallas kernels, attend(): pl.pallas_call(make_attend(first, last, piece_rows, span_rows, kv.shape[0...  113 us
    all_to_all x4, starting transfers between devices, exchange(): return lax.all_to_all(x, axes, split_axis=0, concat_axis=0, tiled=True)  24.5 us
    all_to_all x4, waiting for transfers between devices, exchange(): return lax.all_to_all(x, axes, split_axis=0, concat_axis=0, tiled=True)  24 us
    ppermute x4, waiting for transfers between devices, swap(): return lax.ppermute(x, axis, [(0, 1), (1, 0)])  18.2 us
    all_to_all x1, blocking collectives, exchange(): return lax.all_to_all(x, axes, split_axis=0, concat_axis=0, tiled=True)  16.5 us
    ppermute x4, starting transfers between devices, swap(): return lax.ppermute(x, axis, [(0, 1), (1, 0)])  9.79 us
  transfers between devices with their start and end apart: 8, of which 6 were waited for; matrix products, arithmetic and copies ran while one was open for 2% of the time, Pallas kernels for 26%

profile of v1, /device:TPU:1, one launch (start us, length us, event | category | flops | bytes accessed | tf_op | source)
XLA Modules:
  0.0 217.2 jit_solution(10962502429142370147)
XLA Ops:
  0.0 0.0 copy-start
  0.0 1.0 stack_reshape.10
  1.0 0.2 copy.14
  1.1 0.9 stack_reshape.11
  2.1 0.2 copy.15
  2.2 0.4 pad_maximum_fusion
  2.6 0.8 reshape.87
  3.4 9.0 %all-to-all-start.1 = ((bf16[8,48,256]{2,1,0:T(8,128)(2,1)}), bf16[8,48,256]{2,1,0:T(8,128)(2,1)S(1)}, u32[]{:S(2)}, u32[]{:S(2)}) async-start(bf16[8,48,256]{2,1,0:T(8,128)(2,1)} %bitcast.8), calls=%async_computation.1 | async-start | bytes 393216 | tf_op jit(solution)/shard_map/all_to_all | solution.py:231
  12.4 0.0 copy-done
  12.4 0.9 prep_q.1
  13.4 8.1 %all-to-all-done.1 = bf16[8,48,256]{2,1,0:T(8,128)(2,1)S(1)} async-done(((bf16[8,48,256]{2,1,0:T(8,128)(2,1)}), bf16[8,48,256]{2,1,0:T(8,128)(2,1)S(1)}, u32[]{:S(2)}, u32[]{:S(2)}) %all-to-all-start.1) | async-done | bytes 196640 | tf_op jit(solution)/shard_map/all_to_all | solution.py:231
  21.4 3.5 %all-to-all-start = ((bf16[4,128,384]{2,1,0:T(8,128)(2,1)}), bf16[4,128,384]{2,1,0:T(8,128)(2,1)S(1)}, u32[]{:S(2)}, u32[]{:S(2)}) async-start(bf16[4,128,384]{2,1,0:T(8,128)(2,1)} %prep_q.1), calls=%async_computation | async-start | bytes 786432 | tf_op jit(solution)/shard_map/all_to_all | solution.py:231
  24.9 9.8 %all-to-all-done = bf16[4,128,384]{2,1,0:T(8,128)(2,1)S(1)} async-done(((bf16[4,128,384]{2,1,0:T(8,128)(2,1)}), bf16[4,128,384]{2,1,0:T(8,128)(2,1)S(1)}, u32[]{:S(2)}, u32[]{:S(2)}) %all-to-all-start) | async-done | bytes 393248 | tf_op jit(solution)/shard_map/all_to_all | solution.py:231
  34.7 1.3 broadcast_in_dim.70
  36.0 0.0 copy-start.1
  36.0 6.9 %all-to-all-start.3 = ((bf16[16,192,256]{2,1,0:T(8,128)(2,1)}), bf16[16,192,256]{2,1,0:T(8,128)(2,1)S(1)}, u32[]{:S(2)}, u32[]{:S(2)}) async-start(bf16[16,192,256]{2,1,0:T(8,128)(2,1)} %broadcast_in_dim.70), calls=%async_computation.3 | async-start | bytes 3145728 | tf_op jit(solution)/shard_map/all_to_all | solution.py:231
  42.9 0.0 copy-done.1
  42.9 0.1 stack_reshape.9
  43.0 0.1 reshape.85
  43.1 0.1 copy.13
  43.2 0.1 lt.47
  43.3 0.2 convert_reduce_fusion
  43.5 0.1 collective-permute-start
  43.6 0.1 select_reduce_fusion.2
  43.7 0.8 constant_dynamic-update-slice_fusion.1
  44.5 5.7 %collective-permute-done = bf16[4,128,384]{2,1,0:T(8,128)(2,1)S(1)} collective-permute-done((bf16[4,128,384]{2,1,0:T(8,128)(2,1)S(1)}, bf16[4,128,384]{2,1,0:T(8,128)(2,1)S(1)}, u32[]{:S(2)}, u32[]{:S(2)}) %collective-permute-start) | collective-permute-done | bytes 393248 | tf_op jit(solution)/shard_map/ppermute | solution.py:227
  50.2 0.8 constant_dynamic-update-slice_fusion.refs_7_
  51.0 5.0 %collective-permute-start.1 = (bf16[8,128,384]{2,1,0:T(8,128)(2,1)}, bf16[8,128,384]{2,1,0:T(8,128)(2,1)}, u32[]{:S(2)}, u32[]{:S(2)}) collective-permute-start(bf16[8,128,384]{2,1,0:T(8,128)(2,1)} %constant_dynamic-update-slice_fusion.refs_7_), channel_id=1, source_target_pairs={{0,1},{1,0},{2,3},{3,2},{4,5},{5,4},{6,7},{7,6},{8,9},{9,8},{10,11... | collective-permute-start | bytes 2359304 | tf_op jit(solution)/shard_map/ppermute | solution.py:227
  56.0 0.1 select_reduce_fusion
  56.2 6.2 %all-to-all-done.3 = bf16[16,192,256]{2,1,0:T(8,128)(2,1)S(1)} async-done(((bf16[16,192,256]{2,1,0:T(8,128)(2,1)}), bf16[16,192,256]{2,1,0:T(8,128)(2,1)S(1)}, u32[]{:S(2)}, u32[]{:S(2)}) %all-to-all-start.3) | async-done | bytes 1572896 | tf_op jit(solution)/shard_map/all_to_all | solution.py:231
  62.3 1.3 broadcast_in_dim.68
  63.6 5.1 %all-to-all-start.2 = ((bf16[16,192,256]{2,1,0:T(8,128)(2,1)}), bf16[16,192,256]{2,1,0:T(8,128)(2,1)S(1)}, u32[]{:S(2)}, u32[]{:S(2)}) async-start(bf16[16,192,256]{2,1,0:T(8,128)(2,1)} %broadcast_in_dim.68), calls=%async_computation.2 | async-start | bytes 3145728 | tf_op jit(solution)/shard_map/all_to_all | solution.py:231
  68.8 0.1 pad_add_fusion.1.refs_4_
  68.9 0.2 convert_reduce_fusion.1
  69.1 0.0 collective-permute-done.1.refs_8_
  69.1 56.6 %attend_more.1 = (f32[8,128,768]{2,1,0:T(8,128)}, f32[8,1,768]{2,1,0:T(1,128)S(1)}, f32[8,1,768]{2,1,0:T(1,128)S(1)}) custom-call(s32[69]{0:T(128)S(1)} %get-tuple-element.31.refs_0_, s32[69]{0:T(128)S(1)} %get-tuple-element.36.refs_1_, s32[8]{0:T(128)S(1)} %get-tuple-element.38.refs_2_, s32[8]{0:T(128)S(1)} %get-tuple-element.25.refs_3_, ...), custom_call_target="tpu_custom_call" | custom-call | flops 9663676416 | bytes 1572864 | tf_op jit(solution)/shard_map/attend_more/pallas_call | solution.py:154
  125.7 0.0 all-to-all-done.2
  125.7 56.3 %attend_last.1 = (bf16[8,136,384]{2,1,0:T(8,128)(2,1)S(1)}, bf16[8,136,384]{2,1,0:T(8,128)(2,1)S(1)}) custom-call(s32[69]{0:T(128)S(1)} %get-tuple-element.32.refs_0_, s32[69]{0:T(128)S(1)} %get-tuple-element.35.refs_1_, s32[8]{0:T(128)S(1)} %get-tuple-element.37.refs_2_, s32[8]{0:T(128)S(1)} %get-tuple-element.26.refs_3_, s32[8]{0:T(128)S(1)} %pad_add_fusion.1.refs_4_, ...), custom_call_target="tpu_custom_call" | custom-call | flops 9663676416 | bytes 1572864 | tf_op jit(solution)/shard_map/attend_last/pallas_call | solution.py:154
  182.0 4.2 %collective-permute-start.2 = (bf16[8,136,384]{2,1,0:T(8,128)(2,1)S(1)}, bf16[8,136,384]{2,1,0:T(8,128)(2,1)S(1)}, u32[]{:S(2)}, u32[]{:S(2)}) collective-permute-start(bf16[8,136,384]{2,1,0:T(8,128)(2,1)S(1)} %get-tuple-element.16), channel_id=1, source_target_pairs={{0,1},{1,0},{2,3},{3,2},{4,5},{5,4},{6,7},{7,6},{8,9},{9,8},{10,11... | collective-permute-start | bytes 2506760 | tf_op jit(solution)/shard_map/ppermute | solution.py:227
  186.3 2.0 collective-permute-done.2.b_ref
  188.3 0.5 combine_cores.1
  188.7 0.4 collective-permute-start.3
  189.2 10.5 %collective-permute-done.3.b_ref = bf16[4,136,384]{2,1,0:T(8,128)(2,1)S(1)} collective-permute-done((bf16[4,136,384]{2,1,0:T(8,128)(2,1)S(1)}, bf16[4,136,384]{2,1,0:T(8,128)(2,1)S(1)}, u32[]{:S(2)}, u32[]{:S(2)}) %collective-permute-start.3) | collective-permute-done | bytes 417824 | tf_op jit(solution)/shard_map/ppermute | solution.py:227
  199.7 0.3 combine_chips.1
  199.9 16.5 %all_to_all.25 = bf16[4,96,512]{2,1,0:T(8,128)(2,1)S(1)} all-to-all(bf16[4,96,512]{2,1,0:T(8,128)(2,1)S(1)} %combine_chips.1), channel_id=1, replica_groups=mesh['zh'=4,'y'=4,'x'=4,'zl'=2,'c'=2] {'zh'}, dimensions={0} | all-to-all | bytes 786432 | tf_op jit(solution)/shard_map/all_to_all | solution.py:231
  216.4 0.8 copy.17
  (9 shorter events, 0.1 us)
Async XLA Ops:
  0.0 12.4 %copy-start = (bf16[96,2048]{1,0:T(8,128)(2,1)S(1)}, bf16[96,2048]{1,0:T(8,128)(2,1)}, u32[]{:S(2)}) copy-start(bf16[96,2048]{1,0:T(8,128)(2,1)} %q_ref.1) | copy-start | bytes 1179652
  3.4 18.0 %all-to-all-start.1 = ((bf16[8,48,256]{2,1,0:T(8,128)(2,1)}), bf16[8,48,256]{2,1,0:T(8,128)(2,1)S(1)}, u32[]{:S(2)}, u32[]{:S(2)}) async-start(bf16[8,48,256]{2,1,0:T(8,128)(2,1)} %bitcast.8), calls=%async_computation.1 | async-start | bytes 393216 | tf_op jit(solution)/shard_map/all_to_all | solution.py:231
  21.4 13.3 %all-to-all-start = ((bf16[4,128,384]{2,1,0:T(8,128)(2,1)}), bf16[4,128,384]{2,1,0:T(8,128)(2,1)S(1)}, u32[]{:S(2)}, u32[]{:S(2)}) async-start(bf16[4,128,384]{2,1,0:T(8,128)(2,1)} %prep_q.1), calls=%async_computation | async-start | bytes 786432 | tf_op jit(solution)/shard_map/all_to_all | solution.py:231
  36.0 6.9 %copy-start.1 = (s32[64]{0:T(128)S(1)}, s32[64]{0:T(128)}, u32[]{:S(2)}) copy-start(s32[64]{0:T(128)} %param.7) | copy-start | bytes 772
  36.0 26.3 %all-to-all-start.3 = ((bf16[16,192,256]{2,1,0:T(8,128)(2,1)}), bf16[16,192,256]{2,1,0:T(8,128)(2,1)S(1)}, u32[]{:S(2)}, u32[]{:S(2)}) async-start(bf16[16,192,256]{2,1,0:T(8,128)(2,1)} %broadcast_in_dim.70), calls=%async_computation.3 | async-start | bytes 3145728 | tf_op jit(solution)/shard_map/all_to_all | solution.py:231
  43.5 6.7 %collective-permute-start = (bf16[4,128,384]{2,1,0:T(8,128)(2,1)S(1)}, bf16[4,128,384]{2,1,0:T(8,128)(2,1)S(1)}, u32[]{:S(2)}, u32[]{:S(2)}) collective-permute-start(bf16[4,128,384]{2,1,0:T(8,128)(2,1)S(1)} %all-to-all-done), channel_id=1, source_target_pairs={{0,2},{2,0},{1,3},{3,1},{4,6},{6,4},{5,7},{7,5},{8,10},{10,8},{9,1... | collective-permute-start | bytes 1179656 | tf_op jit(solution)/shard_map/ppermute | solution.py:227
  51.0 18.1 %collective-permute-start.1 = (bf16[8,128,384]{2,1,0:T(8,128)(2,1)}, bf16[8,128,384]{2,1,0:T(8,128)(2,1)}, u32[]{:S(2)}, u32[]{:S(2)}) collective-permute-start(bf16[8,128,384]{2,1,0:T(8,128)(2,1)} %constant_dynamic-update-slice_fusion.refs_7_), channel_id=1, source_target_pairs={{0,1},{1,0},{2,3},{3,2},{4,5},{5,4},{6,7},{7,6},{8,9},{9,8},{10,11... | collective-permute-start | bytes 2359304 | tf_op jit(solution)/shard_map/ppermute | solution.py:227
  63.6 62.1 %all-to-all-start.2 = ((bf16[16,192,256]{2,1,0:T(8,128)(2,1)}), bf16[16,192,256]{2,1,0:T(8,128)(2,1)S(1)}, u32[]{:S(2)}, u32[]{:S(2)}) async-start(bf16[16,192,256]{2,1,0:T(8,128)(2,1)} %broadcast_in_dim.68), calls=%async_computation.2 | async-start | bytes 3145728 | tf_op jit(solution)/shard_map/all_to_all | solution.py:231
  182.0 6.2 %collective-permute-start.2 = (bf16[8,136,384]{2,1,0:T(8,128)(2,1)S(1)}, bf16[8,136,384]{2,1,0:T(8,128)(2,1)S(1)}, u32[]{:S(2)}, u32[]{:S(2)}) collective-permute-start(bf16[8,136,384]{2,1,0:T(8,128)(2,1)S(1)} %get-tuple-element.16), channel_id=1, source_target_pairs={{0,1},{1,0},{2,3},{3,2},{4,5},{5,4},{6,7},{7,6},{8,9},{9,8},{10,11... | collective-permute-start | bytes 2506760 | tf_op jit(solution)/shard_map/ppermute | solution.py:227
  188.7 10.9 %collective-permute-start.3 = (bf16[4,136,384]{2,1,0:T(8,128)(2,1)S(1)}, bf16[4,136,384]{2,1,0:T(8,128)(2,1)S(1)}, u32[]{:S(2)}, u32[]{:S(2)}) collective-permute-start(bf16[4,136,384]{2,1,0:T(8,128)(2,1)S(1)} %get-tuple-element.18), channel_id=1, source_target_pairs={{0,2},{2,0},{1,3},{3,1},{4,6},{6,4},{5,7},{7,5},{8,10},{10,8},{9,1... | collective-permute-start | bytes 1253384 | tf_op jit(solution)/shard_map/ppermute | solution.py:227

commit v2 on v1

v2 whole, which is shorter than its diff:
```python
import jax
import jax.numpy as jnp
from jax import lax
from jax.experimental import pallas as pl
from jax.experimental.pallas import tpu as pltpu
from jax.sharding import Mesh
from jax.sharding import PartitionSpec as P

D = 128
HEADS = 4
AXES = ("zh", "y", "x", "zl", "c")
LOG2E = 1.4426950408889634
LOW = -1e30
SCALE = LOG2E * D**-0.5
NB = 5
ROWS_O = 136
GROUPS = ((1, 2), (3,), (0,))
VMEM = pl.BlockSpec(memory_space=pltpu.VMEM)
SMEM = pl.BlockSpec(memory_space=pltpu.SMEM)


def params(mib=20):
    return pltpu.CompilerParams(vmem_limit_bytes=mib * 1024 * 1024)


def split_kernel(k_ref, v_ref, out_ref):
    half = out_ref.shape[1]
    for h in range(4):
        for part in range(2):
            rows = pl.ds(part * half, half)
            out_ref[2 * h + part, :, 0:D] = k_ref[rows, pl.ds(h * D, D)]
            out_ref[2 * h + part, :, D : 2 * D] = v_ref[rows, pl.ds(h * D, D)]


def split_heads(keys, values):
    return pl.pallas_call(
        split_kernel,
        out_shape=jax.ShapeDtypeStruct((8, keys.shape[0] // 2, 2 * D), jnp.bfloat16),
        in_specs=[VMEM] * 2,
        out_specs=VMEM,
        compiler_params=params(),
        name="split_heads",
    )(keys, values)


def turn_kernel(at_ref, q_ref, *out_refs):
    for k, out_ref in enumerate(out_refs):
        head = lax.rem(at_ref[0] + k, 4) * HEADS
        cols = [q_ref[:, pl.ds(pl.multiple_of((head + j) * D, D), D)] for j in range(HEADS)]
        stacked = jnp.concatenate(cols, axis=0).astype(jnp.float32)
        out_ref[...] = jnp.transpose(stacked).astype(jnp.bfloat16)


def turn(at, queries):
    tok = queries.shape[0]
    return pl.pallas_call(
        turn_kernel,
        out_shape=[jax.ShapeDtypeStruct((D, HEADS * tok), jnp.bfloat16)] * 4,
        in_specs=[SMEM, VMEM],
        out_specs=[VMEM] * 4,
        compiler_params=params(),
        name="turn_queries",
    )(at, queries)


def place_kernel(at_ref, *refs):
    out_ref = refs[4]
    width = HEADS * D
    for k in range(4):
        head = lax.rem(at_ref[0] + k, 4)
        out_ref[:, pl.ds(pl.multiple_of(head * width, width), width)] = refs[k][...]


def place(at, blocks):
    tok = blocks[0].shape[0]
    return pl.pallas_call(
        place_kernel,
        out_shape=jax.ShapeDtypeStruct((tok, 4 * HEADS * D), jnp.bfloat16),
        in_specs=[SMEM] + [VMEM] * 4,
        out_specs=VMEM,
        compiler_params=params(),
        name="place_heads",
    )(at, *blocks)


def make_attend(first_unit, units, piece_rows, span_rows, count, width):
    tiles = 2 * width // 256
    tok = span_rows // 2
    padded = count + 2 * NB

    def kernel(table, qa, qb, kv, own_ref, other_ref, acc, m, l, s0, s1, t0, t1):
        at_tab, at_span, at_full, at_all, at_q = 0, padded, 2 * padded, 2 * padded + 8, 2 * padded + 16
        koff, near, away = table[2 * padded + 24], table[2 * padded + 25], table[2 * padded + 26]

        def q_tile(j, t):
            lo = t * 256
            if lo + 256 <= width:
                return qa[j, :, lo : lo + 256]
            if lo >= width:
                return qb[j, :, lo - width : lo - width + 256]
            return jnp.concatenate([qa[j, :, lo:], qb[j, :, : 256 - (width - lo)]], axis=1)

        def rows_of(base):
            return [
                pl.ds(pl.multiple_of(table[at_tab + base + i] * piece_rows, 16), piece_rows) for i in range(NB)
            ]

        def score(j, base, s_ref, top_ref):
            keys = jnp.concatenate([kv[r, 0:D] for r in rows_of(base)], axis=0)
            for t in range(tiles):
                cs = pl.ds(t * 256, 256)
                s = jnp.dot(keys, q_tile(j, t), preferred_element_type=jnp.float32)
                s_ref[:, cs] = s
                top_ref[:, cs] = jnp.max(s, axis=0, keepdims=True)

        def absorb(j, base, s_ref, top_ref, masked):
            vals = jnp.concatenate([kv[r, D : 2 * D] for r in rows_of(base)], axis=0)
            if masked:
                within = lax.broadcasted_iota(jnp.int32, (piece_rows, 256), 0) + koff
                kpos = jnp.concatenate(
                    [within + table[at_span + base + i] * span_rows for i in range(NB)], axis=0
                )
            for t in range(tiles):
                cs = pl.ds(t * 256, 256)
                s = s_ref[:, cs]
                if masked:
                    col = lax.broadcasted_iota(jnp.int32, (1, 256), 1) + t * 256
                    qpos = lax.rem(col, tok) + jnp.where(col < width, near, away) + table[at_q + j] * span_rows
                    ok = kpos <= qpos
                    s = jnp.where(ok, s, LOW)
                    top = jnp.max(s, axis=0, keepdims=True)
                else:
                    top = top_ref[:, cs]
                m_old = m[:, cs]
                m_new = jnp.maximum(m_old, top * SCALE)
                alpha = jnp.exp2(m_old - m_new)
                p = jnp.exp2(s * SCALE - m_new)
                if masked:
                    p = jnp.where(ok, p, 0.0)
                l[:, cs] = l[:, cs] * alpha + jnp.sum(p, axis=0, keepdims=True)
                m[:, cs] = m_new
                pv = lax.dot_general(
                    vals, p.astype(jnp.bfloat16), (((0,), (0,)), ((), ())), preferred_element_type=jnp.float32
                )
                acc[:, cs] = acc[:, cs] * alpha + pv

        def one_span(u, carry):
            j = u + first_unit
            acc[...] = jnp.zeros(acc.shape, jnp.float32)
            m[...] = jnp.full(m.shape, LOW, jnp.float32)
            l[...] = jnp.zeros(l.shape, jnp.float32)
            full = table[at_full + j] // NB
            score(j, 0, s0, t0)

            def step(i, c):
                base = i * (2 * NB)
                score(j, base + NB, s1, t1)
                absorb(j, base, s0, t0, False)
                score(j, base + 2 * NB, s0, t0)
                absorb(j, base + NB, s1, t1, False)
                return c

            lax.fori_loop(0, full // 2, step, 0)
            odd = full % 2 == 1

            @pl.when(odd)
            def _():
                score(j, full * NB, s1, t1)
                absorb(j, full * NB - NB, s0, t0, False)
                absorb(j, full * NB, s1, t1, True)

            @pl.when(jnp.logical_not(odd))
            def _():
                absorb(j, full * NB, s0, t0, True)

            total = l[...]
            seen = total > 0.0
            safe = jnp.where(seen, total, 1.0)
            lse = jnp.where(seen, m[...] + jnp.log2(safe), LOW)
            inv = 1.0 / safe
            hi = lse.astype(jnp.bfloat16).astype(jnp.float32)
            mid = (lse - hi).astype(jnp.bfloat16).astype(jnp.float32)
            stat = jnp.concatenate([hi, mid, lse - hi - mid, jnp.zeros((5, 2 * width), jnp.float32)], axis=0)
            stat = stat.astype(jnp.bfloat16)
            for ref, lo in ((own_ref, 0), (other_ref, width)):
                cs = pl.ds(lo, width)
                ref[u, 0:D] = (acc[:, cs] * inv[:, lo : lo + width]).astype(jnp.bfloat16)
                ref[u, D:ROWS_O] = stat[:, lo : lo + width]
            return carry

        lax.fori_loop(0, units, one_span, 0)

    return kernel


def attend(table, qa, qb, kv, piece_rows, span_rows, group, first, units):
    width = qa.shape[2]
    count = kv.shape[0] // piece_rows
    wide = 2 * width
    flops = 2 * 2 * units * wide * D * kv.shape[0] // 2
    return pl.pallas_call(
        make_attend(first, units, piece_rows, span_rows, count, width),
        out_shape=[jax.ShapeDtypeStruct((units, ROWS_O, width), jnp.bfloat16)] * 2,
        in_specs=[SMEM] + [VMEM] * 3,
        out_specs=[VMEM] * 2,
        scratch_shapes=[
            pltpu.VMEM((D, wide), jnp.float32),
            pltpu.VMEM((1, wide), jnp.float32),
            pltpu.VMEM((1, wide), jnp.float32),
            pltpu.VMEM((NB * piece_rows, wide), jnp.float32),
            pltpu.VMEM((NB * piece_rows, wide), jnp.float32),
            pltpu.VMEM((1, wide), jnp.float32),
            pltpu.VMEM((1, wide), jnp.float32),
        ],
        compiler_params=params(),
        cost_estimate=pl.CostEstimate(flops=flops * 2, bytes_accessed=kv.size * 2, transcendentals=0),
        name="attend" + str(group),
    )(table, qa, qb, kv)


def weights_of(a, b):
    def lse(ref):
        s = ref[D : D + 8].astype(jnp.float32)
        return s[0:1] + s[1:2] + s[2:3]

    la, lb = lse(a), lse(b)
    top = jnp.maximum(la, lb)
    ea, eb = jnp.exp2(la - top), jnp.exp2(lb - top)
    total = ea + eb
    return ea / total, eb / total, top + jnp.log2(total)


def combine_kernel(a_ref, b_ref, keep_ref, send_ref):
    half = keep_ref.shape[0]
    for j in range(a_ref.shape[0]):
        wa, wb, lse = weights_of(a_ref[j], b_ref[j])
        mixed = a_ref[j, 0:D].astype(jnp.float32) * wa + b_ref[j, 0:D].astype(jnp.float32) * wb
        hi = lse.astype(jnp.bfloat16).astype(jnp.float32)
        mid = (lse - hi).astype(jnp.bfloat16).astype(jnp.float32)
        stat = jnp.concatenate([hi, mid, lse - hi - mid, jnp.zeros((5, lse.shape[1]), jnp.float32)], axis=0)
        ref = keep_ref if j < half else send_ref
        ref[j % half, 0:D] = mixed.astype(jnp.bfloat16)
        ref[j % half, D:ROWS_O] = stat.astype(jnp.bfloat16)


def combine(a, b):
    n = a.shape[0] // 2
    shape = jax.ShapeDtypeStruct((n,) + a.shape[1:], jnp.bfloat16)
    return pl.pallas_call(
        combine_kernel,
        out_shape=[shape, shape],
        in_specs=[VMEM] * 2,
        out_specs=[VMEM] * 2,
        compiler_params=params(),
        name="combine_cores",
    )(a, b)


def finish_kernel(a_ref, b_ref, *out_refs):
    tok = out_refs[0].shape[0]
    for j, out_ref in enumerate(out_refs):
        wa, wb, _ = weights_of(a_ref[j], b_ref[j])
        mixed = a_ref[j, 0:D].astype(jnp.float32) * wa + b_ref[j, 0:D].astype(jnp.float32) * wb
        rows = jnp.transpose(mixed).astype(jnp.bfloat16)
        for h in range(HEADS):
            out_ref[:, pl.ds(h * D, D)] = rows[h * tok : (h + 1) * tok]


def finish(a, b):
    tok = a.shape[2] // HEADS
    return pl.pallas_call(
        finish_kernel,
        out_shape=[jax.ShapeDtypeStruct((tok, HEADS * D), jnp.bfloat16)] * a.shape[0],
        in_specs=[VMEM] * 2,
        out_specs=[VMEM] * a.shape[0],
        compiler_params=params(),
        name="combine_chips",
    )(a, b)


def swap(x, axis):
    return lax.ppermute(x, axis, [(0, 1), (1, 0)])


def shift(x, k):
    return lax.ppermute(x, "zh", [(i, (i + k) % 4) for i in range(4)])


def exchange(x, axes):
    return lax.all_to_all(x, axes, split_axis=0, concat_axis=0, tiled=True)


def pick(values, index):
    slots = jnp.arange(values.shape[0], dtype=jnp.int32)
    return jnp.sum(jnp.where(slots[None, :] == index[:, None], values[None, :], 0), axis=1)


def per_device(queries, key_vectors, value_matrix, span_order):
    tok = queries.shape[0]
    pairs = span_order.shape[0]
    span_rows = 2 * tok
    piece = tok // 2
    yx = lax.axis_size("y") * lax.axis_size("x")
    zh, zl, c = (lax.axis_index(a).astype(jnp.int32) for a in ("zh", "zl", "c"))
    mine = lax.axis_index("y").astype(jnp.int32) * lax.axis_size("x") + lax.axis_index("x").astype(jnp.int32)
    at = jnp.stack([zh, zl])

    column = exchange(split_heads(key_vectors, value_matrix), ("zh", "zl"))
    blocks = turn(at, queries)
    spread = jnp.broadcast_to(column.reshape(1, 8 * piece, 2 * D), (yx, 8 * piece, 2 * D))
    spread, blocks = lax.optimization_barrier((spread, blocks))
    gathered = exchange(spread, ("y", "x")).reshape(yx * 8 * piece, 2 * D)

    got = [blocks[0]] + [shift(blocks[k], k) for k in range(1, 4)]
    far = swap(jnp.stack(got), "zl")
    q_near = jnp.stack([b for ks in GROUPS for b in [got[k] for k in ks] + [far[k] for k in ks]])
    q_far = swap(q_near, "c")

    order = span_order.astype(jnp.int32)
    span = jnp.arange(2 * pairs, dtype=jnp.int32)
    early = jnp.minimum(span, 2 * pairs - 1 - span)
    ids = jnp.arange(pairs, dtype=jnp.int32)
    pair = jnp.sum(jnp.where(order[None, :] == early[:, None], ids[None, :], 0), axis=1)
    tab = (pair % yx) * 8 + (pair // yx) * 2 + (span >= pairs)
    behind = (zh - jnp.asarray([k for ks in GROUPS for k in ks + ks], jnp.int32)) % 4
    other = jnp.asarray([f for ks in GROUPS for f in [0] * len(ks) + [1] * len(ks)], jnp.int32)
    here = pick(order, behind * yx + mine)
    q_span = jnp.where(zl == other, here, 2 * pairs - 1 - here)
    pad = jnp.zeros((2 * NB,), jnp.int32)
    scalars = jnp.stack([c * tok + zl * piece, c * tok, (1 - c) * tok])
    table = jnp.concatenate([tab, pad, span, pad + (1 << 16), q_span, q_span + 1, q_span, scalars])

    starts = [2 * sum(len(ks) for ks in GROUPS[:g]) for g in range(len(GROUPS))]
    ends, waiting = {}, []

    def merge(own, other):
        return combine(own, swap(other, "c"))

    def close(ks, keep, send):
        done = finish(keep, swap(send, "zl"))
        for i, k in enumerate(ks):
            ends[k] = done[i] if k == 0 else shift(done[i], 4 - k)

    merged = []
    for g, ks in enumerate(GROUPS):
        part = attend(table, q_near, q_far, gathered, piece, span_rows, g, starts[g], 2 * len(ks))
        waiting.append(part)
        if g == 0:
            table, waiting[0] = lax.optimization_barrier((table, part))
        elif g < len(GROUPS) - 1:
            merged.append(merge(*waiting.pop(0)))
            table, merged[-1], waiting[0] = lax.optimization_barrier((table, merged[-1], waiting[0]))
    merged += [merge(*w) for w in waiting]
    for ks, m in zip(GROUPS, merged):
        close(ks, *m)
    return place(at, [ends[k] for k in range(4)])


def solution(mesh):
    finer = Mesh(mesh.devices.reshape(4, 4, 4, 2, 2), AXES)
    spec = P(AXES, None)
    return jax.shard_map(
        per_device, mesh=finer, in_specs=(spec, spec, spec, P()), out_specs=spec, check_vma=False
    )
```

time: 220 us -> 137 us (0.62)
  Pallas kernels: 115 us -> 41.6 us
  blocking collectives: 16.5 us -> 0 us
  local copies, waits for them, and re-layouts: 8.37 us -> 12.1 us
  starting transfers between devices: 34.3 us -> 36.7 us
    pallas_call x4 -> x9, Pallas kernels: 114 us -> 41.1 us  [the longest x3 37.9 us: attend(): pl.pallas_call(make_attend(first, units, piece_rows, span_rows, count, wi...]
    all_to_all x1 -> x0, blocking collectives: 16.5 us -> none  [exchange(): return lax.all_to_all(x, axes, split_axis=0, concat_axis=0, tiled=True)]
    ppermute x0 -> x6, waiting for transfers between devices: none -> 16 us  [shift(): return lax.ppermute(x, 'zh', [(i, (i + k) % 4) for i in range(4)])]
    ppermute x0 -> x6, starting transfers between devices: none -> 12.7 us  [shift(): return lax.ppermute(x, 'zh', [(i, (i + k) % 4) for i in range(4)])]
    all_to_all x4 -> x2, waiting for transfers between devices: 24 us -> 14.6 us  [exchange(): return lax.all_to_all(x, axes, split_axis=0, concat_axis=0, tiled=True)]
    unnamed x5 -> x16, local copies, waits for them, and re-layouts: 0.81 us -> 9.41 us
    all_to_all x4 -> x2, starting transfers between devices: 24.5 us -> 15.9 us  [exchange(): return lax.all_to_all(x, axes, split_axis=0, concat_axis=0, tiled=True)]
    ppermute x4 -> x8, waiting for transfers between devices: 18.2 us -> 11.6 us  [swap(): return lax.ppermute(x, axis, [(0, 1), (1, 0)])]
  transfers between devices with their start and end apart: 8 -> 16, of which waited for: 6 -> 10; matrix products, arithmetic and copies ran while one was open for 2% -> 7% of each run, Pallas kernels for 26% -> 16%
where the time goes in v2:
time: 137 us; the launch traced here: 136 us
  waiting for transfers between devices  42.2 us (31%)
  Pallas kernels  41.6 us (30%)
  starting transfers between devices  36.7 us (27%)
  local copies, waits for them, and re-layouts  12.1 us (9%)
  other arithmetic  2.74 us (2%)
    pallas_call x3, Pallas kernels, attend(): pl.pallas_call(make_attend(first, units, piece_rows, span_rows, count, wi...  37.9 us
    ppermute x6, waiting for transfers between devices, shift(): return lax.ppermute(x, 'zh', [(i, (i + k) % 4) for i in range(4)])  16 us
    all_to_all x2, starting transfers between devices, exchange(): return lax.all_to_all(x, axes, split_axis=0, concat_axis=0, tiled=True)  15.9 us
    all_to_all x2, waiting for transfers between devices, exchange(): return lax.all_to_all(x, axes, split_axis=0, concat_axis=0, tiled=True)  14.6 us
    ppermute x6, starting transfers between devices, shift(): return lax.ppermute(x, 'zh', [(i, (i + k) % 4) for i in range(4)])  12.7 us
    ppermute x8, waiting for transfers between devices, swap(): return lax.ppermute(x, axis, [(0, 1), (1, 0)])  11.6 us
    unnamed x16, local copies, waits for them, and re-layouts  9.41 us
    ppermute x8, starting transfers between devices, swap(): return lax.ppermute(x, axis, [(0, 1), (1, 0)])  8.18 us
  transfers between devices with their start and end apart: 16, of which 10 were waited for; matrix products, arithmetic and copies ran while one was open for 7% of the time, Pallas kernels for 16%

profile of v2, /device:TPU:1, one launch (start us, length us, event | category | flops | bytes accessed | tf_op | source)
XLA Modules:
  0.0 135.6 jit_solution(15262711632456675030)
XLA Ops:
  0.0 0.0 copy-start.1
  0.0 0.9 copy-done.1
  0.9 0.0 copy-start.2
  0.9 0.9 copy-done.2
  1.8 0.7 split_heads.1
  2.5 9.0 %all-to-all-start = ((bf16[8,48,256]{2,1,0:T(8,128)(2,1)}), bf16[8,48,256]{2,1,0:T(8,128)(2,1)S(1)}, u32[]{:S(2)}, u32[]{:S(2)}) async-start(bf16[8,48,256]{2,1,0:T(8,128)(2,1)} %split_heads.1), calls=%async_computation | async-start | bytes 393216 | tf_op jit(solution)/shard_map/all_to_all | solution.py:290
  11.5 0.1 pad_add_fusion.at_ref
  11.6 1.0 copy-done
  12.6 0.7 turn_queries.1
  13.3 7.2 %all-to-all-done = bf16[8,48,256]{2,1,0:T(8,128)(2,1)S(1)} async-done(((bf16[8,48,256]{2,1,0:T(8,128)(2,1)}), bf16[8,48,256]{2,1,0:T(8,128)(2,1)S(1)}, u32[]{:S(2)}, u32[]{:S(2)}) %all-to-all-start) | async-done | bytes 196640 | tf_op jit(solution)/shard_map/all_to_all | solution.py:290
  20.5 1.9 %broadcast_in_dim.42 = bf16[16,384,256]{2,1,0:T(8,128)(2,1)} broadcast(bf16[384,256]{1,0:T(8,128)(2,1)S(1)} %bitcast.19), dimensions={1,2} | broadcast | bytes 3342336 | tf_op jit(solution)/shard_map/broadcast_in_dim | solution.py:310
  22.4 6.9 %all-to-all-start.1 = ((bf16[16,384,256]{2,1,0:T(8,128)(2,1)}), bf16[16,384,256]{2,1,0:T(8,128)(2,1)S(1)}, u32[]{:S(2)}, u32[]{:S(2)}) async-start(bf16[16,384,256]{2,1,0:T(8,128)(2,1)} %broadcast_in_dim.42), calls=%async_computation.1 | async-start | bytes 6291456 | tf_op jit(solution)/shard_map/all_to_all | solution.py:290
  29.3 0.1 collective-permute-start
  29.4 3.3 %collective-permute-start.1 = (bf16[128,384]{1,0:T(8,128)(2,1)S(1)}, bf16[128,384]{1,0:T(8,128)(2,1)}, u32[]{:S(2)}, u32[]{:S(2)}) collective-permute-start(bf16[128,384]{1,0:T(8,128)(2,1)S(1)} %get-tuple-element.41), channel_id=1, source_target_pairs={{0,128},{64,192},{128,0},{192,64},{1,129},{65,193},{129,1},{193,65... | collective-permute-start | bytes 294920 | tf_op jit(solution)/shard_map/ppermute | solution.py:286
  32.7 1.9 %collective-permute-start.2 = (bf16[128,384]{1,0:T(8,128)(2,1)S(1)}, bf16[128,384]{1,0:T(8,128)(2,1)}, u32[]{:S(2)}, u32[]{:S(2)}) collective-permute-start(bf16[128,384]{1,0:T(8,128)(2,1)S(1)} %get-tuple-element.43), channel_id=1, source_target_pairs={{0,192},{64,0},{128,64},{192,128},{1,193},{65,1},{129,65},{193,129... | collective-permute-start | bytes 294920 | tf_op jit(solution)/shard_map/ppermute | solution.py:286
  34.7 0.0 copy-done.4
  34.7 1.5 %collective-permute-done = bf16[128,384]{1,0:T(8,128)(2,1)} collective-permute-done((bf16[128,384]{1,0:T(8,128)(2,1)S(1)}, bf16[128,384]{1,0:T(8,128)(2,1)}, u32[]{:S(2)}, u32[]{:S(2)}) %collective-permute-start) | collective-permute-done | bytes 98336 | tf_op jit(solution)/shard_map/ppermute | solution.py:286
  36.1 3.1 %collective-permute-done.1 = bf16[128,384]{1,0:T(8,128)(2,1)} collective-permute-done((bf16[128,384]{1,0:T(8,128)(2,1)S(1)}, bf16[128,384]{1,0:T(8,128)(2,1)}, u32[]{:S(2)}, u32[]{:S(2)}) %collective-permute-start.1) | collective-permute-done | bytes 98336 | tf_op jit(solution)/shard_map/ppermute | solution.py:286
  39.3 4.7 %collective-permute-done.2 = bf16[128,384]{1,0:T(8,128)(2,1)} collective-permute-done((bf16[128,384]{1,0:T(8,128)(2,1)S(1)}, bf16[128,384]{1,0:T(8,128)(2,1)}, u32[]{:S(2)}, u32[]{:S(2)}) %collective-permute-start.2) | collective-permute-done | bytes 98336 | tf_op jit(solution)/shard_map/ppermute | solution.py:286
  43.9 1.0 pad_maximum_fusion
  45.0 0.1 collective-permute-start.3
  45.1 1.5 %constant_dynamic-update-slice_fusion.3 = bf16[8,128,384]{2,1,0:T(8,128)(2,1)} fusion(bf16[128,384]{1,0:T(8,128)(2,1)} %collective-permute-done), kind=kLoop, calls=%fused_computation.8 | loop fusion | bytes 196608
  46.6 1.6 %constant_dynamic-update-slice_fusion.2 = bf16[8,128,384]{2,1,0:T(8,128)(2,1)} fusion(bf16[8,128,384]{2,1,0:T(8,128)(2,1)} %constant_dynamic-update-slice_fusion.3, bf16[128,384]{1,0:T(8,128)(2,1)} %collective-permute-done.1), kind=kLoop, calls=%fused_computation.7 | loop fusion | bytes 196608
  48.2 6.6 %collective-permute-done.3 = bf16[4,128,384]{2,1,0:T(8,128)(2,1)S(1)} collective-permute-done((bf16[4,128,384]{2,1,0:T(8,128)(2,1)S(1)}, bf16[4,128,384]{2,1,0:T(8,128)(2,1)S(1)}, u32[]{:S(2)}, u32[]{:S(2)}) %collective-permute-start.3) | collective-permute-done | bytes 393248 | tf_op jit(solution)/shard_map/ppermute | solution.py:282
  54.8 0.7 slice_dynamic-update-slice_fusion
  55.5 1.5 %constant_dynamic-update-slice_fusion.1 = bf16[8,128,384]{2,1,0:T(8,128)(2,1)} fusion(bf16[8,128,384]{2,1,0:T(8,128)(2,1)} %slice_dynamic-update-slice_fusion, bf16[128,384]{1,0:T(8,128)(2,1)} %collective-permute-done.2), kind=kLoop, calls=%fused_computation.6 | loop fusion | bytes 196608
  57.0 0.6 slice_dynamic-update-slice_fusion.2
  57.7 0.7 constant_dynamic-update-slice_fusion
  58.3 0.7 slice_dynamic-update-slice_fusion.1.qa
  59.0 1.8 %collective-permute-start.4 = (bf16[8,128,384]{2,1,0:T(8,128)(2,1)}, bf16[8,128,384]{2,1,0:T(8,128)(2,1)}, u32[]{:S(2)}, u32[]{:S(2)}) collective-permute-start(bf16[8,128,384]{2,1,0:T(8,128)(2,1)} %slice_dynamic-update-slice_fusion.1.qa), channel_id=1, source_target_pairs={{0,1},{1,0},{2,3},{3,2},{4,5},{5,4},{6,7},{7,6},{8,9},{9,8},{10,11... | collective-permute-start | bytes 2359304 | tf_op jit(solution)/shard_map/ppermute | solution.py:282
  60.8 0.8 select_reduce_fusion.1
  61.7 0.7 select_reduce_fusion
  62.4 0.0 copy-done.3
  62.5 0.1 concatenate.3.table
  62.6 0.5 collective-permute-done.4.qb
  63.1 7.4 %all-to-all-done.1 = bf16[16,384,256]{2,1,0:T(8,128)(2,1)S(1)} async-done(((bf16[16,384,256]{2,1,0:T(8,128)(2,1)}), bf16[16,384,256]{2,1,0:T(8,128)(2,1)S(1)}, u32[]{:S(2)}, u32[]{:S(2)}) %all-to-all-start.1) | async-done | bytes 3145760 | tf_op jit(solution)/shard_map/all_to_all | solution.py:290
  70.5 18.1 %attend0.1 = (bf16[4,136,384]{2,1,0:T(8,128)(2,1)S(1)}, bf16[4,136,384]{2,1,0:T(8,128)(2,1)S(1)}) custom-call(s32[303]{0:T(512)S(1)} %concatenate.3.table, bf16[8,128,384]{2,1,0:T(8,128)(2,1)} %slice_dynamic-update-slice_fusion.1.qa, bf16[8,128,384]{2,1,0:T(8,128)(2,1)} %collective-permute-done.4.qb, bf16[6144,256]{1,0:T(8,128)(2,1)S(1)} %bitcast.15), custom_call_target="tpu_custom_call" | custom-call | flops 9663676416 | bytes 3145728 | tf_op jit(solution)/shard_map/attend0/pallas_call | solution.py:201
  88.6 3.9 %collective-permute-start.5 = (bf16[4,136,384]{2,1,0:T(8,128)(2,1)S(1)}, bf16[4,136,384]{2,1,0:T(8,128)(2,1)S(1)}, u32[]{:S(2)}, u32[]{:S(2)}) collective-permute-start(bf16[4,136,384]{2,1,0:T(8,128)(2,1)S(1)} %get-tuple-element.49), channel_id=1, source_target_pairs={{0,1},{1,0},{2,3},{3,2},{4,5},{5,4},{6,7},{7,6},{8,9},{9,8},{10,11... | collective-permute-start | bytes 1253384 | tf_op jit(solution)/shard_map/ppermute | solution.py:282
  92.5 9.9 %attend1.1 = (bf16[2,136,384]{2,1,0:T(8,128)(2,1)S(1)}, bf16[2,136,384]{2,1,0:T(8,128)(2,1)S(1)}) custom-call(s32[303]{0:T(512)S(1)} %concatenate.3.table, bf16[8,128,384]{2,1,0:T(8,128)(2,1)} %slice_dynamic-update-slice_fusion.1.qa, bf16[8,128,384]{2,1,0:T(8,128)(2,1)} %collective-permute-done.4.qb, bf16[6144,256]{1,0:T(8,128)(2,1)S(1)} %bitcast.16), custom_call_target="tpu_custom_call" | custom-call | flops 4831838208 | bytes 3145728 | tf_op jit(solution)/shard_map/attend1/pallas_call | solution.py:201
  102.4 0.0 collective-permute-done.5.b_ref
  102.4 0.3 combine_cores.3
  102.6 0.1 collective-permute-start.11
  102.7 9.9 %attend2.1 = (bf16[2,136,384]{2,1,0:T(8,128)(2,1)S(1)}, bf16[2,136,384]{2,1,0:T(8,128)(2,1)S(1)}) custom-call(s32[303]{0:T(512)S(1)} %concatenate.3.table, bf16[8,128,384]{2,1,0:T(8,128)(2,1)} %slice_dynamic-update-slice_fusion.1.qa, bf16[8,128,384]{2,1,0:T(8,128)(2,1)} %collective-permute-done.4.qb, bf16[6144,256]{1,0:T(8,128)(2,1)S(1)} %bitcast.17), custom_call_target="tpu_custom_call" | custom-call | flops 4831838208 | bytes 3145728 | tf_op jit(solution)/shard_map/attend2/pallas_call | solution.py:201
  112.7 0.6 collective-permute-start.6
  113.2 0.0 collective-permute-start.8
  113.2 0.0 collective-permute-done.11.b_ref
  113.2 0.1 combine_cores.5
  113.4 1.5 %collective-permute-start.12 = (bf16[1,136,384]{2,1,0:T(8,128)(2,1)S(1)}, bf16[1,136,384]{2,1,0:T(8,128)(2,1)S(1)}, u32[]{:S(2)}, u32[]{:S(2)}) collective-permute-start(bf16[1,136,384]{2,1,0:T(8,128)(2,1)S(1)} %get-tuple-element.66), channel_id=1, source_target_pairs={{0,2},{2,0},{1,3},{3,1},{4,6},{6,4},{5,7},{7,5},{8,10},{10,8},{9,1... | collective-permute-start | bytes 313352 | tf_op jit(solution)/shard_map/ppermute | solution.py:282
  114.9 0.0 collective-permute-done.6.b_ref
  114.9 0.1 combine_cores.4
  115.1 0.1 collective-permute-start.7
  115.2 4.5 %collective-permute-done.8.b_ref = bf16[2,136,384]{2,1,0:T(8,128)(2,1)S(1)} collective-permute-done((bf16[2,136,384]{2,1,0:T(8,128)(2,1)S(1)}, bf16[2,136,384]{2,1,0:T(8,128)(2,1)S(1)}, u32[]{:S(2)}, u32[]{:S(2)}) %collective-permute-start.8) | collective-permute-done | bytes 208928 | tf_op jit(solution)/shard_map/ppermute | solution.py:282
  119.7 0.2 combine_chips.4
  119.9 4.2 %collective-permute-start.9 = (bf16[96,512]{1,0:T(8,128)(2,1)S(1)}, bf16[96,512]{1,0:T(8,128)(2,1)S(1)}, u32[]{:S(2)}, u32[]{:S(2)}) collective-permute-start(bf16[96,512]{1,0:T(8,128)(2,1)S(1)} %get-tuple-element.61), channel_id=1, source_target_pairs={{0,192},{64,0},{128,64},{192,128},{1,193},{65,1},{129,65},{193,129... | collective-permute-start | bytes 294920 | tf_op jit(solution)/shard_map/ppermute | solution.py:286
  124.0 0.8 collective-permute-start.10
  124.9 0.0 collective-permute-done.12.b_ref
  124.9 0.1 combine_chips.5
  125.0 2.3 %collective-permute-start.13 = (bf16[96,512]{1,0:T(8,128)(2,1)S(1)}, bf16[96,512]{1,0:T(8,128)(2,1)S(1)}, u32[]{:S(2)}, u32[]{:S(2)}) collective-permute-start(bf16[96,512]{1,0:T(8,128)(2,1)S(1)} %combine_chips.5), channel_id=1, source_target_pairs={{0,64},{64,128},{128,192},{192,0},{1,65},{65,129},{129,193},{193,1... | collective-permute-start | bytes 294920 | tf_op jit(solution)/shard_map/ppermute | solution.py:286
  127.3 0.0 collective-permute-done.7.b_ref
  127.3 0.1 combine_chips.3.refs_0_
  127.5 0.0 collective-permute-done.9.refs_1_
  127.5 4.1 %collective-permute-done.10.refs_2_ = bf16[96,512]{1,0:T(8,128)(2,1)S(1)} collective-permute-done((bf16[96,512]{1,0:T(8,128)(2,1)S(1)}, bf16[96,512]{1,0:T(8,128)(2,1)S(1)}, u32[]{:S(2)}, u32[]{:S(2)}) %collective-permute-start.10) | collective-permute-done | bytes 98336 | tf_op jit(solution)/shard_map/ppermute | solution.py:286
  131.6 2.6 %collective-permute-done.13.refs_3_ = bf16[96,512]{1,0:T(8,128)(2,1)S(1)} collective-permute-done((bf16[96,512]{1,0:T(8,128)(2,1)S(1)}, bf16[96,512]{1,0:T(8,128)(2,1)S(1)}, u32[]{:S(2)}, u32[]{:S(2)}) %collective-permute-start.13) | collective-permute-done | bytes 98336 | tf_op jit(solution)/shard_map/ppermute | solution.py:286
  134.2 1.3 place_heads.1
  (10 shorter events, 0.1 us)
Async XLA Ops:
  0.0 0.9 copy-start.1
  0.9 0.9 copy-start.2
  2.5 18.0 %all-to-all-start = ((bf16[8,48,256]{2,1,0:T(8,128)(2,1)}), bf16[8,48,256]{2,1,0:T(8,128)(2,1)S(1)}, u32[]{:S(2)}, u32[]{:S(2)}) async-start(bf16[8,48,256]{2,1,0:T(8,128)(2,1)} %split_heads.1), calls=%async_computation | async-start | bytes 393216 | tf_op jit(solution)/shard_map/all_to_all | solution.py:290
  11.6 1.0 copy-start
  22.4 12.2 %copy-start.4 = (s32[8]{0:T(128)S(1)}, s32[8]{0:T(128)}, u32[]{:S(2)}) copy-start(s32[8]{0:T(128)} %constant.89) | copy-start | bytes 100
  22.4 40.0 %copy-start.3 = (s32[8]{0:T(128)S(1)}, s32[8]{0:T(128)}, u32[]{:S(2)}) copy-start(s32[8]{0:T(128)} %constant.85.clone) | copy-start | bytes 100
  22.4 48.0 %all-to-all-start.1 = ((bf16[16,384,256]{2,1,0:T(8,128)(2,1)}), bf16[16,384,256]{2,1,0:T(8,128)(2,1)S(1)}, u32[]{:S(2)}, u32[]{:S(2)}) async-start(bf16[16,384,256]{2,1,0:T(8,128)(2,1)} %broadcast_in_dim.42), calls=%async_computation.1 | async-start | bytes 6291456 | tf_op jit(solution)/shard_map/all_to_all | solution.py:290
  29.3 6.8 %collective-permute-start = (bf16[128,384]{1,0:T(8,128)(2,1)S(1)}, bf16[128,384]{1,0:T(8,128)(2,1)}, u32[]{:S(2)}, u32[]{:S(2)}) collective-permute-start(bf16[128,384]{1,0:T(8,128)(2,1)S(1)} %get-tuple-element.40), channel_id=1, source_target_pairs={{0,64},{64,128},{128,192},{192,0},{1,65},{65,129},{129,193},{193,1... | collective-permute-start | bytes 294920 | tf_op jit(solution)/shard_map/ppermute | solution.py:286
  29.4 9.9 %collective-permute-start.1 = (bf16[128,384]{1,0:T(8,128)(2,1)S(1)}, bf16[128,384]{1,0:T(8,128)(2,1)}, u32[]{:S(2)}, u32[]{:S(2)}) collective-permute-start(bf16[128,384]{1,0:T(8,128)(2,1)S(1)} %get-tuple-element.41), channel_id=1, source_target_pairs={{0,128},{64,192},{128,0},{192,64},{1,129},{65,193},{129,1},{193,65... | collective-permute-start | bytes 294920 | tf_op jit(solution)/shard_map/ppermute | solution.py:286
  32.7 11.2 %collective-permute-start.2 = (bf16[128,384]{1,0:T(8,128)(2,1)S(1)}, bf16[128,384]{1,0:T(8,128)(2,1)}, u32[]{:S(2)}, u32[]{:S(2)}) collective-permute-start(bf16[128,384]{1,0:T(8,128)(2,1)S(1)} %get-tuple-element.43), channel_id=1, source_target_pairs={{0,192},{64,0},{128,64},{192,128},{1,193},{65,1},{129,65},{193,129... | collective-permute-start | bytes 294920 | tf_op jit(solution)/shard_map/ppermute | solution.py:286
  45.0 9.8 %collective-permute-start.3 = (bf16[4,128,384]{2,1,0:T(8,128)(2,1)S(1)}, bf16[4,128,384]{2,1,0:T(8,128)(2,1)S(1)}, u32[]{:S(2)}, u32[]{:S(2)}) collective-permute-start(bf16[4,128,384]{2,1,0:T(8,128)(2,1)S(1)} %pad_maximum_fusion), channel_id=1, source_target_pairs={{0,2},{2,0},{1,3},{3,1},{4,6},{6,4},{5,7},{7,5},{8,10},{10,8},{9,1... | collective-permute-start | bytes 1179656 | tf_op jit(solution)/shard_map/ppermute | solution.py:282
  59.0 4.1 %collective-permute-start.4 = (bf16[8,128,384]{2,1,0:T(8,128)(2,1)}, bf16[8,128,384]{2,1,0:T(8,128)(2,1)}, u32[]{:S(2)}, u32[]{:S(2)}) collective-permute-start(bf16[8,128,384]{2,1,0:T(8,128)(2,1)} %slice_dynamic-update-slice_fusion.1.qa), channel_id=1, source_target_pairs={{0,1},{1,0},{2,3},{3,2},{4,5},{5,4},{6,7},{7,6},{8,9},{9,8},{10,11... | collective-permute-start | bytes 2359304 | tf_op jit(solution)/shard_map/ppermute | solution.py:282
  88.6 13.8 %collective-permute-start.5 = (bf16[4,136,384]{2,1,0:T(8,128)(2,1)S(1)}, bf16[4,136,384]{2,1,0:T(8,128)(2,1)S(1)}, u32[]{:S(2)}, u32[]{:S(2)}) collective-permute-start(bf16[4,136,384]{2,1,0:T(8,128)(2,1)S(1)} %get-tuple-element.49), channel_id=1, source_target_pairs={{0,1},{1,0},{2,3},{3,2},{4,5},{5,4},{6,7},{7,6},{8,9},{9,8},{10,11... | collective-permute-start | bytes 1253384 | tf_op jit(solution)/shard_map/ppermute | solution.py:282
  102.6 10.6 %collective-permute-start.11 = (bf16[2,136,384]{2,1,0:T(8,128)(2,1)S(1)}, bf16[2,136,384]{2,1,0:T(8,128)(2,1)S(1)}, u32[]{:S(2)}, u32[]{:S(2)}) collective-permute-start(bf16[2,136,384]{2,1,0:T(8,128)(2,1)S(1)} %get-tuple-element.64), channel_id=1, source_target_pairs={{0,1},{1,0},{2,3},{3,2},{4,5},{5,4},{6,7},{7,6},{8,9},{9,8},{10,11... | collective-permute-start | bytes 626696 | tf_op jit(solution)/shard_map/ppermute | solution.py:282
  112.7 2.3 %collective-permute-start.6 = (bf16[2,136,384]{2,1,0:T(8,128)(2,1)S(1)}, bf16[2,136,384]{2,1,0:T(8,128)(2,1)S(1)}, u32[]{:S(2)}, u32[]{:S(2)}) collective-permute-start(bf16[2,136,384]{2,1,0:T(8,128)(2,1)S(1)} %get-tuple-element.56), channel_id=1, source_target_pairs={{0,1},{1,0},{2,3},{3,2},{4,5},{5,4},{6,7},{7,6},{8,9},{9,8},{10,11... | collective-permute-start | bytes 626696 | tf_op jit(solution)/shard_map/ppermute | solution.py:282
  113.2 6.4 %collective-permute-start.8 = (bf16[2,136,384]{2,1,0:T(8,128)(2,1)S(1)}, bf16[2,136,384]{2,1,0:T(8,128)(2,1)S(1)}, u32[]{:S(2)}, u32[]{:S(2)}) collective-permute-start(bf16[2,136,384]{2,1,0:T(8,128)(2,1)S(1)} %get-tuple-element.60), channel_id=1, source_target_pairs={{0,2},{2,0},{1,3},{3,1},{4,6},{6,4},{5,7},{7,5},{8,10},{10,8},{9,1... | collective-permute-start | bytes 626696 | tf_op jit(solution)/shard_map/ppermute | solution.py:282
  113.4 11.5 %collective-permute-start.12 = (bf16[1,136,384]{2,1,0:T(8,128)(2,1)S(1)}, bf16[1,136,384]{2,1,0:T(8,128)(2,1)S(1)}, u32[]{:S(2)}, u32[]{:S(2)}) collective-permute-start(bf16[1,136,384]{2,1,0:T(8,128)(2,1)S(1)} %get-tuple-element.66), channel_id=1, source_target_pairs={{0,2},{2,0},{1,3},{3,1},{4,6},{6,4},{5,7},{7,5},{8,10},{10,8},{9,1... | collective-permute-start | bytes 313352 | tf_op jit(solution)/shard_map/ppermute | solution.py:282
  115.1 12.3 %collective-permute-start.7 = (bf16[1,136,384]{2,1,0:T(8,128)(2,1)S(1)}, bf16[1,136,384]{2,1,0:T(8,128)(2,1)S(1)}, u32[]{:S(2)}, u32[]{:S(2)}) collective-permute-start(bf16[1,136,384]{2,1,0:T(8,128)(2,1)S(1)} %get-tuple-element.58), channel_id=1, source_target_pairs={{0,2},{2,0},{1,3},{3,1},{4,6},{6,4},{5,7},{7,5},{8,10},{10,8},{9,1... | collective-permute-start | bytes 313352 | tf_op jit(solution)/shard_map/ppermute | solution.py:282
  119.9 7.6 %collective-permute-start.9 = (bf16[96,512]{1,0:T(8,128)(2,1)S(1)}, bf16[96,512]{1,0:T(8,128)(2,1)S(1)}, u32[]{:S(2)}, u32[]{:S(2)}) collective-permute-start(bf16[96,512]{1,0:T(8,128)(2,1)S(1)} %get-tuple-element.61), channel_id=1, source_target_pairs={{0,192},{64,0},{128,64},{192,128},{1,193},{65,1},{129,65},{193,129... | collective-permute-start | bytes 294920 | tf_op jit(solution)/shard_map/ppermute | solution.py:286
  124.0 7.6 %collective-permute-start.10 = (bf16[96,512]{1,0:T(8,128)(2,1)S(1)}, bf16[96,512]{1,0:T(8,128)(2,1)S(1)}, u32[]{:S(2)}, u32[]{:S(2)}) collective-permute-start(bf16[96,512]{1,0:T(8,128)(2,1)S(1)} %get-tuple-element.62), channel_id=1, source_target_pairs={{0,128},{64,192},{128,0},{192,64},{1,129},{65,193},{129,1},{193,65... | collective-permute-start | bytes 294920 | tf_op jit(solution)/shard_map/ppermute | solution.py:286
  125.0 9.2 %collective-permute-start.13 = (bf16[96,512]{1,0:T(8,128)(2,1)S(1)}, bf16[96,512]{1,0:T(8,128)(2,1)S(1)}, u32[]{:S(2)}, u32[]{:S(2)}) collective-permute-start(bf16[96,512]{1,0:T(8,128)(2,1)S(1)} %combine_chips.5), channel_id=1, source_target_pairs={{0,64},{64,128},{128,192},{192,0},{1,65},{65,129},{129,193},{193,1... | collective-permute-start | bytes 294920 | tf_op jit(solution)/shard_map/ppermute | solution.py:286

commit v3 on v2

--- a/solution.py
+++ b/solution.py
@@ -14,7 +14,7 @@
 SCALE = LOG2E * D**-0.5
 NB = 5
 ROWS_O = 136
-GROUPS = ((1, 2), (3,), (0,))
+GROUPS = ((2,), (1,), (3,), (0,))
 VMEM = pl.BlockSpec(memory_space=pltpu.VMEM)
 SMEM = pl.BlockSpec(memory_space=pltpu.SMEM)
 
@@ -89,7 +89,7 @@
     padded = count + 2 * NB
 
     def kernel(table, qa, qb, kv, own_ref, other_ref, acc, m, l, s0, s1, t0, t1):
-        at_tab, at_span, at_full, at_all, at_q = 0, padded, 2 * padded, 2 * padded + 8, 2 * padded + 16
+        at_tab, at_span, at_full, at_q = 0, padded, 2 * padded, 2 * padded + 16
         koff, near, away = table[2 * padded + 24], table[2 * padded + 25], table[2 * padded + 26]
 
         def q_tile(j, t):
@@ -193,7 +193,7 @@
     return kernel
 
 
-def attend(table, qa, qb, kv, piece_rows, span_rows, group, first, units):
+def attend(table, qa, qb, kv, piece_rows, span_rows, first, units):
     width = qa.shape[2]
     count = kv.shape[0] // piece_rows
     wide = 2 * width
@@ -214,7 +214,6 @@
         ],
         compiler_params=params(),
         cost_estimate=pl.CostEstimate(flops=flops * 2, bytes_accessed=kv.size * 2, transcendentals=0),
-        name="attend" + str(group),
     )(table, qa, qb, kv)
 
 
@@ -309,7 +308,8 @@
     blocks = turn(at, queries)
     spread = jnp.broadcast_to(column.reshape(1, 8 * piece, 2 * D), (yx, 8 * piece, 2 * D))
     spread, blocks = lax.optimization_barrier((spread, blocks))
-    gathered = exchange(spread, ("y", "x")).reshape(yx * 8 * piece, 2 * D)
+    gathered = exchange(spread, ("y", "x"))
+    gathered = gathered.reshape(yx * 8 * piece, 2 * D)
 
     got = [blocks[0]] + [shift(blocks[k], k) for k in range(1, 4)]
     far = swap(jnp.stack(got), "zl")
@@ -330,29 +330,14 @@
     scalars = jnp.stack([c * tok + zl * piece, c * tok, (1 - c) * tok])
     table = jnp.concatenate([tab, pad, span, pad + (1 << 16), q_span, q_span + 1, q_span, scalars])
 
-    starts = [2 * sum(len(ks) for ks in GROUPS[:g]) for g in range(len(GROUPS))]
-    ends, waiting = {}, []
-
-    def merge(own, other):
-        return combine(own, swap(other, "c"))
-
-    def close(ks, keep, send):
+    ends, first = {}, 0
+    for ks in GROUPS:
+        own, other = attend(table, q_near, q_far, gathered, piece, span_rows, first, 2 * len(ks))
+        first += 2 * len(ks)
+        keep, send = combine(own, swap(other, "c"))
         done = finish(keep, swap(send, "zl"))
         for i, k in enumerate(ks):
             ends[k] = done[i] if k == 0 else shift(done[i], 4 - k)
-
-    merged = []
-    for g, ks in enumerate(GROUPS):
-        part = attend(table, q_near, q_far, gathered, piece, span_rows, g, starts[g], 2 * len(ks))
-        waiting.append(part)
-        if g == 0:
-            table, waiting[0] = lax.optimization_barrier((table, part))
-        elif g < len(GROUPS) - 1:
-            merged.append(merge(*waiting.pop(0)))
-            table, merged[-1], waiting[0] = lax.optimization_barrier((table, merged[-1], waiting[0]))
-    merged += [merge(*w) for w in waiting]
-    for ks, m in zip(GROUPS, merged):
-        close(ks, *m)
     return place(at, [ends[k] for k in range(4)])
 
 

time: 137 us -> 142 us (1.036)
  waiting for transfers between devices: 42.2 us -> 50.2 us
  starting transfers between devices: 36.7 us -> 34.7 us
    all_to_all x2, waiting for transfers between devices: 14.6 us -> 28.3 us  [exchange(): return lax.all_to_all(x, axes, split_axis=0, concat_axis=0, tiled=True)]
    ppermute x6, waiting for transfers between devices: 16 us -> 9.25 us  [shift(): return lax.ppermute(x, 'zh', [(i, (i + k) % 4) for i in range(4)])]
    ppermute x6, starting transfers between devices: 12.7 us -> 8.54 us  [shift(): return lax.ppermute(x, 'zh', [(i, (i + k) % 4) for i in range(4)])]
    ppermute x8 -> x10, starting transfers between devices: 8.18 us -> 10.3 us  [swap(): return lax.ppermute(x, axis, [(0, 1), (1, 0)])]
    ppermute x8 -> x10, waiting for transfers between devices: 11.6 us -> 12.6 us  [swap(): return lax.ppermute(x, axis, [(0, 1), (1, 0)])]
    unnamed x16 -> x19, local copies, waits for them, and re-layouts: 9.41 us -> 10 us
    pallas_call x3 -> x4, Pallas kernels: 37.9 us -> 38.5 us  [attend(): pl.pallas_call(make_attend(first, units, piece_rows, span_rows, count, wi...]
  transfers between devices with their start and end apart: 16 -> 18, of which waited for: 10 -> 11; matrix products, arithmetic and copies ran while one was open for 7% -> 7% of each run, Pallas kernels for 16% -> 22%
where the time goes in v3:
time: 142 us
  waiting for transfers between devices  50.2 us (35%)
  Pallas kernels  42.3 us (30%)
  starting transfers between devices  34.7 us (24%)
  local copies, waits for them, and re-layouts  12.7 us (9%)
  other arithmetic  1.44 us (1%)
    pallas_call x4, Pallas kernels, attend(): pl.pallas_call(make_attend(first, units, piece_rows, span_rows, count, wi...  38.5 us
    all_to_all x2, waiting for transfers between devices, exchange(): return lax.all_to_all(x, axes, split_axis=0, concat_axis=0, tiled=True)  28.3 us
    all_to_all x2, starting transfers between devices, exchange(): return lax.all_to_all(x, axes, split_axis=0, concat_axis=0, tiled=True)  15.9 us
    ppermute x10, waiting for transfers between devices, swap(): return lax.ppermute(x, axis, [(0, 1), (1, 0)])  12.6 us
    ppermute x10, starting transfers between devices, swap(): return lax.ppermute(x, axis, [(0, 1), (1, 0)])  10.3 us
    unnamed x19, local copies, waits for them, and re-layouts  10 us
    ppermute x6, waiting for transfers between devices, shift(): return lax.ppermute(x, 'zh', [(i, (i + k) % 4) for i in range(4)])  9.25 us
    ppermute x6, starting transfers between devices, shift(): return lax.ppermute(x, 'zh', [(i, (i + k) % 4) for i in range(4)])  8.54 us
  transfers between devices with their start and end apart: 18, of which 11 were waited for; matrix products, arithmetic and copies ran while one was open for 7% of the time, Pallas kernels for 22%

profile of v3, /device:TPU:1, one launch (start us, length us, event | category | flops | bytes accessed | tf_op | source)
XLA Modules:
  0.0 141.6 jit_solution(10660551259894265090)
XLA Ops:
  0.0 0.9 copy-done.1
  0.9 0.9 copy-done.2
  1.8 0.7 split_heads.1
  2.5 9.0 %all-to-all-start = ((bf16[8,48,256]{2,1,0:T(8,128)(2,1)}), bf16[8,48,256]{2,1,0:T(8,128)(2,1)S(1)}, u32[]{:S(2)}, u32[]{:S(2)}) async-start(bf16[8,48,256]{2,1,0:T(8,128)(2,1)} %split_heads.1), calls=%async_computation | async-start | bytes 393216 | tf_op jit(solution)/shard_map/all_to_all | solution.py:289
  11.5 0.1 pad_add_fusion.at_ref
  11.6 1.0 copy-done
  12.6 0.7 turn_queries.1
  13.3 7.2 %all-to-all-done = bf16[8,48,256]{2,1,0:T(8,128)(2,1)S(1)} async-done(((bf16[8,48,256]{2,1,0:T(8,128)(2,1)}), bf16[8,48,256]{2,1,0:T(8,128)(2,1)S(1)}, u32[]{:S(2)}, u32[]{:S(2)}) %all-to-all-start) | async-done | bytes 196640 | tf_op jit(solution)/shard_map/all_to_all | solution.py:289
  20.5 1.9 %broadcast_in_dim.42 = bf16[16,384,256]{2,1,0:T(8,128)(2,1)} broadcast(bf16[384,256]{1,0:T(8,128)(2,1)S(1)} %bitcast.20), dimensions={1,2} | broadcast | bytes 3342336 | tf_op jit(solution)/shard_map/broadcast_in_dim | solution.py:309
  22.4 1.7 %collective-permute-start = (bf16[128,384]{1,0:T(8,128)(2,1)S(1)}, bf16[128,384]{1,0:T(8,128)(2,1)}, u32[]{:S(2)}, u32[]{:S(2)}) collective-permute-start(bf16[128,384]{1,0:T(8,128)(2,1)S(1)} %get-tuple-element.34), channel_id=1, source_target_pairs={{0,128},{64,192},{128,0},{192,64},{1,129},{65,193},{129,1},{193,65... | collective-permute-start | bytes 294920 | tf_op jit(solution)/shard_map/ppermute | solution.py:285
  24.1 1.6 %collective-permute-start.1 = (bf16[128,384]{1,0:T(8,128)(2,1)S(1)}, bf16[128,384]{1,0:T(8,128)(2,1)}, u32[]{:S(2)}, u32[]{:S(2)}) collective-permute-start(bf16[128,384]{1,0:T(8,128)(2,1)S(1)} %get-tuple-element.36), channel_id=1, source_target_pairs={{0,64},{64,128},{128,192},{192,0},{1,65},{65,129},{129,193},{193,1... | collective-permute-start | bytes 294920 | tf_op jit(solution)/shard_map/ppermute | solution.py:285
  25.8 1.9 %collective-permute-start.2 = (bf16[128,384]{1,0:T(8,128)(2,1)S(1)}, bf16[128,384]{1,0:T(8,128)(2,1)}, u32[]{:S(2)}, u32[]{:S(2)}) collective-permute-start(bf16[128,384]{1,0:T(8,128)(2,1)S(1)} %get-tuple-element.37), channel_id=1, source_target_pairs={{0,192},{64,0},{128,64},{192,128},{1,193},{65,1},{129,65},{193,129... | collective-permute-start | bytes 294920 | tf_op jit(solution)/shard_map/ppermute | solution.py:285
  27.7 6.9 %all-to-all-start.1 = ((bf16[16,384,256]{2,1,0:T(8,128)(2,1)}), bf16[16,384,256]{2,1,0:T(8,128)(2,1)S(1)}, u32[]{:S(2)}, u32[]{:S(2)}) async-start(bf16[16,384,256]{2,1,0:T(8,128)(2,1)} %broadcast_in_dim.42), calls=%async_computation.1 | async-start | bytes 6291456 | tf_op jit(solution)/shard_map/all_to_all | solution.py:289
  34.6 0.0 collective-permute-done
  34.6 0.0 collective-permute-done.1
  34.6 0.4 collective-permute-done.2
  35.0 1.0 pad_maximum_fusion
  36.1 0.1 collective-permute-start.3
  36.2 1.5 %constant_dynamic-update-slice_fusion.3 = bf16[8,128,384]{2,1,0:T(8,128)(2,1)} fusion(bf16[128,384]{1,0:T(8,128)(2,1)} %collective-permute-done), kind=kLoop, calls=%fused_computation.9 | loop fusion | bytes 196608
  37.8 7.4 %collective-permute-done.3 = bf16[4,128,384]{2,1,0:T(8,128)(2,1)S(1)} collective-permute-done((bf16[4,128,384]{2,1,0:T(8,128)(2,1)S(1)}, bf16[4,128,384]{2,1,0:T(8,128)(2,1)S(1)}, u32[]{:S(2)}, u32[]{:S(2)}) %collective-permute-start.3) | collective-permute-done | bytes 393248 | tf_op jit(solution)/shard_map/ppermute | solution.py:281
  45.1 0.7 slice_dynamic-update-slice_fusion.3
  45.8 1.5 %constant_dynamic-update-slice_fusion.2 = bf16[8,128,384]{2,1,0:T(8,128)(2,1)} fusion(bf16[8,128,384]{2,1,0:T(8,128)(2,1)} %slice_dynamic-update-slice_fusion.3, bf16[128,384]{1,0:T(8,128)(2,1)} %collective-permute-done.1), kind=kLoop, calls=%fused_computation.8 | loop fusion | bytes 196608
  47.3 0.7 slice_dynamic-update-slice_fusion.2
  48.0 1.5 %constant_dynamic-update-slice_fusion.1 = bf16[8,128,384]{2,1,0:T(8,128)(2,1)} fusion(bf16[8,128,384]{2,1,0:T(8,128)(2,1)} %slice_dynamic-update-slice_fusion.2, bf16[128,384]{1,0:T(8,128)(2,1)} %collective-permute-done.2), kind=kLoop, calls=%fused_computation.7 | loop fusion | bytes 196608
  49.5 0.6 slice_dynamic-update-slice_fusion.1
  50.2 0.6 constant_dynamic-update-slice_fusion
  50.8 0.6 slice_dynamic-update-slice_fusion.qa
  51.5 2.6 %collective-permute-start.4 = (bf16[8,128,384]{2,1,0:T(8,128)(2,1)}, bf16[8,128,384]{2,1,0:T(8,128)(2,1)}, u32[]{:S(2)}, u32[]{:S(2)}) collective-permute-start(bf16[8,128,384]{2,1,0:T(8,128)(2,1)} %slice_dynamic-update-slice_fusion.qa), channel_id=1, source_target_pairs={{0,1},{1,0},{2,3},{3,2},{4,5},{5,4},{6,7},{7,6},{8,9},{9,8},{10,11... | collective-permute-start | bytes 2359304 | tf_op jit(solution)/shard_map/ppermute | solution.py:281
  54.1 0.2 select_reduce_fusion.1
  54.2 0.1 select_reduce_fusion
  54.4 0.1 concatenate.3.table
  54.5 1.8 %collective-permute-done.4.qb = bf16[8,128,384]{2,1,0:T(8,128)(2,1)} collective-permute-done((bf16[8,128,384]{2,1,0:T(8,128)(2,1)}, bf16[8,128,384]{2,1,0:T(8,128)(2,1)}, u32[]{:S(2)}, u32[]{:S(2)}) %collective-permute-start.4) | collective-permute-done | bytes 786464 | tf_op jit(solution)/shard_map/ppermute | solution.py:281
  56.3 21.2 %all-to-all-done.1 = bf16[16,384,256]{2,1,0:T(8,128)(2,1)S(1)} async-done(((bf16[16,384,256]{2,1,0:T(8,128)(2,1)}), bf16[16,384,256]{2,1,0:T(8,128)(2,1)S(1)}, u32[]{:S(2)}, u32[]{:S(2)}) %all-to-all-start.1) | async-done | bytes 3145760 | tf_op jit(solution)/shard_map/all_to_all | solution.py:289
  77.5 9.6 %shard_map.67 = (bf16[2,136,384]{2,1,0:T(8,128)(2,1)S(1)}, bf16[2,136,384]{2,1,0:T(8,128)(2,1)S(1)}) custom-call(s32[303]{0:T(512)S(1)} %concatenate.3.table, bf16[8,128,384]{2,1,0:T(8,128)(2,1)} %slice_dynamic-update-slice_fusion.qa, bf16[8,128,384]{2,1,0:T(8,128)(2,1)} %collective-permute-done.4.qb, bf16[6144,256]{1,0:T(8,128)(2,1)S(1)} %bitcast.15), custom_call_target="tpu_custom_call" | custom-call | flops 4831838208 | bytes 3145728 | tf_op jit(solution)/shard_map/pallas_call | solution.py:201
  87.1 3.4 %collective-permute-start.13 = (bf16[2,136,384]{2,1,0:T(8,128)(2,1)S(1)}, bf16[2,136,384]{2,1,0:T(8,128)(2,1)S(1)}, u32[]{:S(2)}, u32[]{:S(2)}) collective-permute-start(bf16[2,136,384]{2,1,0:T(8,128)(2,1)S(1)} %get-tuple-element.52), channel_id=1, source_target_pairs={{0,1},{1,0},{2,3},{3,2},{4,5},{5,4},{6,7},{7,6},{8,9},{9,8},{10,11... | collective-permute-start | bytes 626696 | tf_op jit(solution)/shard_map/ppermute | solution.py:281
  90.4 9.6 %shard_map.66 = (bf16[2,136,384]{2,1,0:T(8,128)(2,1)S(1)}, bf16[2,136,384]{2,1,0:T(8,128)(2,1)S(1)}) custom-call(s32[303]{0:T(512)S(1)} %concatenate.3.table, bf16[8,128,384]{2,1,0:T(8,128)(2,1)} %slice_dynamic-update-slice_fusion.qa, bf16[8,128,384]{2,1,0:T(8,128)(2,1)} %collective-permute-done.4.qb, bf16[6144,256]{1,0:T(8,128)(2,1)S(1)} %bitcast.16), custom_call_target="tpu_custom_call" | custom-call | flops 4831838208 | bytes 3145728 | tf_op jit(solution)/shard_map/pallas_call | solution.py:201
  100.1 0.1 collective-permute-start.10
  100.2 9.6 %shard_map.65 = (bf16[2,136,384]{2,1,0:T(8,128)(2,1)S(1)}, bf16[2,136,384]{2,1,0:T(8,128)(2,1)S(1)}) custom-call(s32[303]{0:T(512)S(1)} %concatenate.3.table, bf16[8,128,384]{2,1,0:T(8,128)(2,1)} %slice_dynamic-update-slice_fusion.qa, bf16[8,128,384]{2,1,0:T(8,128)(2,1)} %collective-permute-done.4.qb, bf16[6144,256]{1,0:T(8,128)(2,1)S(1)} %bitcast.17), custom_call_target="tpu_custom_call" | custom-call | flops 4831838208 | bytes 3145728 | tf_op jit(solution)/shard_map/pallas_call | solution.py:201
  109.8 0.8 collective-permute-start.7
  110.6 9.6 %shard_map.64 = (bf16[2,136,384]{2,1,0:T(8,128)(2,1)S(1)}, bf16[2,136,384]{2,1,0:T(8,128)(2,1)S(1)}) custom-call(s32[303]{0:T(512)S(1)} %concatenate.3.table, bf16[8,128,384]{2,1,0:T(8,128)(2,1)} %slice_dynamic-update-slice_fusion.qa, bf16[8,128,384]{2,1,0:T(8,128)(2,1)} %collective-permute-done.4.qb, bf16[6144,256]{1,0:T(8,128)(2,1)S(1)} %bitcast.18), custom_call_target="tpu_custom_call" | custom-call | flops 4831838208 | bytes 3145728 | tf_op jit(solution)/shard_map/pallas_call | solution.py:201
  120.2 0.1 collective-permute-start.5
  120.3 0.0 collective-permute-done.13.b_ref
  120.3 0.1 combine_cores.7
  120.5 0.1 collective-permute-start.14
  120.6 0.1 combine_cores.6
  120.7 1.5 %collective-permute-start.11 = (bf16[1,136,384]{2,1,0:T(8,128)(2,1)S(1)}, bf16[1,136,384]{2,1,0:T(8,128)(2,1)S(1)}, u32[]{:S(2)}, u32[]{:S(2)}) collective-permute-start(bf16[1,136,384]{2,1,0:T(8,128)(2,1)S(1)} %get-tuple-element.50), channel_id=1, source_target_pairs={{0,2},{2,0},{1,3},{3,1},{4,6},{6,4},{5,7},{7,5},{8,10},{10,8},{9,1... | collective-permute-start | bytes 313352 | tf_op jit(solution)/shard_map/ppermute | solution.py:281
  122.2 0.1 combine_cores.5
  122.4 0.1 collective-permute-start.8
  122.5 0.1 combine_cores.4
  122.7 1.5 %collective-permute-start.6 = (bf16[1,136,384]{2,1,0:T(8,128)(2,1)S(1)}, bf16[1,136,384]{2,1,0:T(8,128)(2,1)S(1)}, u32[]{:S(2)}, u32[]{:S(2)}) collective-permute-start(bf16[1,136,384]{2,1,0:T(8,128)(2,1)S(1)} %get-tuple-element.42), channel_id=1, source_target_pairs={{0,2},{2,0},{1,3},{3,1},{4,6},{6,4},{5,7},{7,5},{8,10},{10,8},{9,1... | collective-permute-start | bytes 313352 | tf_op jit(solution)/shard_map/ppermute | solution.py:281
  124.2 0.3 collective-permute-done.14.b_ref
  124.5 0.1 combine_chips.7
  124.7 0.1 collective-permute-start.15
  124.8 2.0 %collective-permute-done.11.b_ref = bf16[1,136,384]{2,1,0:T(8,128)(2,1)S(1)} collective-permute-done((bf16[1,136,384]{2,1,0:T(8,128)(2,1)S(1)}, bf16[1,136,384]{2,1,0:T(8,128)(2,1)S(1)}, u32[]{:S(2)}, u32[]{:S(2)}) %collective-permute-start.11) | collective-permute-done | bytes 104480 | tf_op jit(solution)/shard_map/ppermute | solution.py:281
  126.8 0.1 combine_chips.6
  126.9 1.8 %collective-permute-start.12 = (bf16[96,512]{1,0:T(8,128)(2,1)S(1)}, bf16[96,512]{1,0:T(8,128)(2,1)S(1)}, u32[]{:S(2)}, u32[]{:S(2)}) collective-permute-start(bf16[96,512]{1,0:T(8,128)(2,1)S(1)} %combine_chips.6), channel_id=1, source_target_pairs={{0,128},{64,192},{128,0},{192,64},{1,129},{65,193},{129,1},{193,65... | collective-permute-start | bytes 294920 | tf_op jit(solution)/shard_map/ppermute | solution.py:285
  128.7 0.3 collective-permute-done.8.b_ref
  129.0 0.1 combine_chips.5
  129.2 1.4 collective-permute-start.9
  130.5 0.8 collective-permute-done.6.b_ref
  131.3 0.1 combine_chips.4.refs_0_
  131.4 2.5 %collective-permute-done.15.refs_3_ = bf16[96,512]{1,0:T(8,128)(2,1)S(1)} collective-permute-done((bf16[96,512]{1,0:T(8,128)(2,1)S(1)}, bf16[96,512]{1,0:T(8,128)(2,1)S(1)}, u32[]{:S(2)}, u32[]{:S(2)}) %collective-permute-start.15) | collective-permute-done | bytes 98336 | tf_op jit(solution)/shard_map/ppermute | solution.py:285
  133.9 6.3 %collective-permute-done.12.refs_2_ = bf16[96,512]{1,0:T(8,128)(2,1)S(1)} collective-permute-done((bf16[96,512]{1,0:T(8,128)(2,1)S(1)}, bf16[96,512]{1,0:T(8,128)(2,1)S(1)}, u32[]{:S(2)}, u32[]{:S(2)}) %collective-permute-start.12) | collective-permute-done | bytes 98336 | tf_op jit(solution)/shard_map/ppermute | solution.py:285
  140.2 1.3 place_heads.1
  (20 shorter events, 0.1 us)
Async XLA Ops:
  0.0 0.9 copy-start.1
  0.9 0.9 copy-start.2
  2.5 18.0 %all-to-all-start = ((bf16[8,48,256]{2,1,0:T(8,128)(2,1)}), bf16[8,48,256]{2,1,0:T(8,128)(2,1)S(1)}, u32[]{:S(2)}, u32[]{:S(2)}) async-start(bf16[8,48,256]{2,1,0:T(8,128)(2,1)} %split_heads.1), calls=%async_computation | async-start | bytes 393216 | tf_op jit(solution)/shard_map/all_to_all | solution.py:289
  11.6 1.0 copy-start
  22.4 12.2 %collective-permute-start = (bf16[128,384]{1,0:T(8,128)(2,1)S(1)}, bf16[128,384]{1,0:T(8,128)(2,1)}, u32[]{:S(2)}, u32[]{:S(2)}) collective-permute-start(bf16[128,384]{1,0:T(8,128)(2,1)S(1)} %get-tuple-element.34), channel_id=1, source_target_pairs={{0,128},{64,192},{128,0},{192,64},{1,129},{65,193},{129,1},{193,65... | collective-permute-start | bytes 294920 | tf_op jit(solution)/shard_map/ppermute | solution.py:285
  24.1 10.5 %collective-permute-start.1 = (bf16[128,384]{1,0:T(8,128)(2,1)S(1)}, bf16[128,384]{1,0:T(8,128)(2,1)}, u32[]{:S(2)}, u32[]{:S(2)}) collective-permute-start(bf16[128,384]{1,0:T(8,128)(2,1)S(1)} %get-tuple-element.36), channel_id=1, source_target_pairs={{0,64},{64,128},{128,192},{192,0},{1,65},{65,129},{129,193},{193,1... | collective-permute-start | bytes 294920 | tf_op jit(solution)/shard_map/ppermute | solution.py:285
  25.8 9.3 %collective-permute-start.2 = (bf16[128,384]{1,0:T(8,128)(2,1)S(1)}, bf16[128,384]{1,0:T(8,128)(2,1)}, u32[]{:S(2)}, u32[]{:S(2)}) collective-permute-start(bf16[128,384]{1,0:T(8,128)(2,1)S(1)} %get-tuple-element.37), channel_id=1, source_target_pairs={{0,192},{64,0},{128,64},{192,128},{1,193},{65,1},{129,65},{193,129... | collective-permute-start | bytes 294920 | tf_op jit(solution)/shard_map/ppermute | solution.py:285
  27.7 8.5 %copy-start.4 = (s32[8]{0:T(128)S(1)}, s32[8]{0:T(128)}, u32[]{:S(2)}) copy-start(s32[8]{0:T(128)} %constant.89) | copy-start | bytes 100
  27.7 26.4 %copy-start.5 = (s32[64]{0:T(128)S(1)}, s32[64]{0:T(128)}, u32[]{:S(2)}) copy-start(s32[64]{0:T(128)} %param.9) | copy-start | bytes 772
  27.7 26.7 %copy-start.3 = (s32[8]{0:T(128)S(1)}, s32[8]{0:T(128)}, u32[]{:S(2)}) copy-start(s32[8]{0:T(128)} %constant.85.clone) | copy-start | bytes 100
  27.7 49.8 %all-to-all-start.1 = ((bf16[16,384,256]{2,1,0:T(8,128)(2,1)}), bf16[16,384,256]{2,1,0:T(8,128)(2,1)S(1)}, u32[]{:S(2)}, u32[]{:S(2)}) async-start(bf16[16,384,256]{2,1,0:T(8,128)(2,1)} %broadcast_in_dim.42), calls=%async_computation.1 | async-start | bytes 6291456 | tf_op jit(solution)/shard_map/all_to_all | solution.py:289
  36.1 9.0 %collective-permute-start.3 = (bf16[4,128,384]{2,1,0:T(8,128)(2,1)S(1)}, bf16[4,128,384]{2,1,0:T(8,128)(2,1)S(1)}, u32[]{:S(2)}, u32[]{:S(2)}) collective-permute-start(bf16[4,128,384]{2,1,0:T(8,128)(2,1)S(1)} %pad_maximum_fusion), channel_id=1, source_target_pairs={{0,2},{2,0},{1,3},{3,1},{4,6},{6,4},{5,7},{7,5},{8,10},{10,8},{9,1... | collective-permute-start | bytes 1179656 | tf_op jit(solution)/shard_map/ppermute | solution.py:281
  51.5 4.8 %collective-permute-start.4 = (bf16[8,128,384]{2,1,0:T(8,128)(2,1)}, bf16[8,128,384]{2,1,0:T(8,128)(2,1)}, u32[]{:S(2)}, u32[]{:S(2)}) collective-permute-start(bf16[8,128,384]{2,1,0:T(8,128)(2,1)} %slice_dynamic-update-slice_fusion.qa), channel_id=1, source_target_pairs={{0,1},{1,0},{2,3},{3,2},{4,5},{5,4},{6,7},{7,6},{8,9},{9,8},{10,11... | collective-permute-start | bytes 2359304 | tf_op jit(solution)/shard_map/ppermute | solution.py:281
  87.1 33.2 %collective-permute-start.13 = (bf16[2,136,384]{2,1,0:T(8,128)(2,1)S(1)}, bf16[2,136,384]{2,1,0:T(8,128)(2,1)S(1)}, u32[]{:S(2)}, u32[]{:S(2)}) collective-permute-start(bf16[2,136,384]{2,1,0:T(8,128)(2,1)S(1)} %get-tuple-element.52), channel_id=1, source_target_pairs={{0,1},{1,0},{2,3},{3,2},{4,5},{5,4},{6,7},{7,6},{8,9},{9,8},{10,11... | collective-permute-start | bytes 626696 | tf_op jit(solution)/shard_map/ppermute | solution.py:281
  100.1 20.5 %collective-permute-start.10 = (bf16[2,136,384]{2,1,0:T(8,128)(2,1)S(1)}, bf16[2,136,384]{2,1,0:T(8,128)(2,1)S(1)}, u32[]{:S(2)}, u32[]{:S(2)}) collective-permute-start(bf16[2,136,384]{2,1,0:T(8,128)(2,1)S(1)} %get-tuple-element.48), channel_id=1, source_target_pairs={{0,1},{1,0},{2,3},{3,2},{4,5},{5,4},{6,7},{7,6},{8,9},{9,8},{10,11... | collective-permute-start | bytes 626696 | tf_op jit(solution)/shard_map/ppermute | solution.py:281
  109.8 12.4 %collective-permute-start.7 = (bf16[2,136,384]{2,1,0:T(8,128)(2,1)S(1)}, bf16[2,136,384]{2,1,0:T(8,128)(2,1)S(1)}, u32[]{:S(2)}, u32[]{:S(2)}) collective-permute-start(bf16[2,136,384]{2,1,0:T(8,128)(2,1)S(1)} %get-tuple-element.44), channel_id=1, source_target_pairs={{0,1},{1,0},{2,3},{3,2},{4,5},{5,4},{6,7},{7,6},{8,9},{9,8},{10,11... | collective-permute-start | bytes 626696 | tf_op jit(solution)/shard_map/ppermute | solution.py:281
  120.2 2.3 %collective-permute-start.5 = (bf16[2,136,384]{2,1,0:T(8,128)(2,1)S(1)}, bf16[2,136,384]{2,1,0:T(8,128)(2,1)S(1)}, u32[]{:S(2)}, u32[]{:S(2)}) collective-permute-start(bf16[2,136,384]{2,1,0:T(8,128)(2,1)S(1)} %get-tuple-element.40), channel_id=1, source_target_pairs={{0,1},{1,0},{2,3},{3,2},{4,5},{5,4},{6,7},{7,6},{8,9},{9,8},{10,11... | collective-permute-start | bytes 626696 | tf_op jit(solution)/shard_map/ppermute | solution.py:281
  120.5 4.1 %collective-permute-start.14 = (bf16[1,136,384]{2,1,0:T(8,128)(2,1)S(1)}, bf16[1,136,384]{2,1,0:T(8,128)(2,1)S(1)}, u32[]{:S(2)}, u32[]{:S(2)}) collective-permute-start(bf16[1,136,384]{2,1,0:T(8,128)(2,1)S(1)} %get-tuple-element.54), channel_id=1, source_target_pairs={{0,2},{2,0},{1,3},{3,1},{4,6},{6,4},{5,7},{7,5},{8,10},{10,8},{9,1... | collective-permute-start | bytes 313352 | tf_op jit(solution)/shard_map/ppermute | solution.py:281
  120.7 6.1 %collective-permute-start.11 = (bf16[1,136,384]{2,1,0:T(8,128)(2,1)S(1)}, bf16[1,136,384]{2,1,0:T(8,128)(2,1)S(1)}, u32[]{:S(2)}, u32[]{:S(2)}) collective-permute-start(bf16[1,136,384]{2,1,0:T(8,128)(2,1)S(1)} %get-tuple-element.50), channel_id=1, source_target_pairs={{0,2},{2,0},{1,3},{3,1},{4,6},{6,4},{5,7},{7,5},{8,10},{10,8},{9,1... | collective-permute-start | bytes 313352 | tf_op jit(solution)/shard_map/ppermute | solution.py:281
  122.4 6.6 %collective-permute-start.8 = (bf16[1,136,384]{2,1,0:T(8,128)(2,1)S(1)}, bf16[1,136,384]{2,1,0:T(8,128)(2,1)S(1)}, u32[]{:S(2)}, u32[]{:S(2)}) collective-permute-start(bf16[1,136,384]{2,1,0:T(8,128)(2,1)S(1)} %get-tuple-element.46), channel_id=1, source_target_pairs={{0,2},{2,0},{1,3},{3,1},{4,6},{6,4},{5,7},{7,5},{8,10},{10,8},{9,1... | collective-permute-start | bytes 313352 | tf_op jit(solution)/shard_map/ppermute | solution.py:281
  122.7 8.6 %collective-permute-start.6 = (bf16[1,136,384]{2,1,0:T(8,128)(2,1)S(1)}, bf16[1,136,384]{2,1,0:T(8,128)(2,1)S(1)}, u32[]{:S(2)}, u32[]{:S(2)}) collective-permute-start(bf16[1,136,384]{2,1,0:T(8,128)(2,1)S(1)} %get-tuple-element.42), channel_id=1, source_target_pairs={{0,2},{2,0},{1,3},{3,1},{4,6},{6,4},{5,7},{7,5},{8,10},{10,8},{9,1... | collective-permute-start | bytes 313352 | tf_op jit(solution)/shard_map/ppermute | solution.py:281
  124.7 9.2 %collective-permute-start.15 = (bf16[96,512]{1,0:T(8,128)(2,1)S(1)}, bf16[96,512]{1,0:T(8,128)(2,1)S(1)}, u32[]{:S(2)}, u32[]{:S(2)}) collective-permute-start(bf16[96,512]{1,0:T(8,128)(2,1)S(1)} %combine_chips.7), channel_id=1, source_target_pairs={{0,64},{64,128},{128,192},{192,0},{1,65},{65,129},{129,193},{193,1... | collective-permute-start | bytes 294920 | tf_op jit(solution)/shard_map/ppermute | solution.py:285
  126.9 13.3 %collective-permute-start.12 = (bf16[96,512]{1,0:T(8,128)(2,1)S(1)}, bf16[96,512]{1,0:T(8,128)(2,1)S(1)}, u32[]{:S(2)}, u32[]{:S(2)}) collective-permute-start(bf16[96,512]{1,0:T(8,128)(2,1)S(1)} %combine_chips.6), channel_id=1, source_target_pairs={{0,128},{64,192},{128,0},{192,64},{1,129},{65,193},{129,1},{193,65... | collective-permute-start | bytes 294920 | tf_op jit(solution)/shard_map/ppermute | solution.py:285
  129.2 11.1 %collective-permute-start.9 = (bf16[96,512]{1,0:T(8,128)(2,1)S(1)}, bf16[96,512]{1,0:T(8,128)(2,1)S(1)}, u32[]{:S(2)}, u32[]{:S(2)}) collective-permute-start(bf16[96,512]{1,0:T(8,128)(2,1)S(1)} %combine_chips.5), channel_id=1, source_target_pairs={{0,192},{64,0},{128,64},{192,128},{1,193},{65,1},{129,65},{193,129... | collective-permute-start | bytes 294920 | tf_op jit(solution)/shard_map/ppermute | solution.py:285
